TPU v7x, 32 devices: a whole 2x2x4 slice. The times are simulated.
32 devices in a mesh: grp: 8 (over y, x, core), own: 4 (over z).
Axes of the slice: x: 2, y: 2, z: 4, core: 2. Of those that a mesh axis runs over, the one named last changes fastest.
Arguments:
- background: bfloat16 [64, 1024, 512], P('grp', 'own'), may hold values from -6 to 6
- obs_ens: bfloat16 [64, 2048, 512], P('grp', 'own'), may hold values from -12 to 12
- innovation: bfloat16 [64, 2048], P('grp', 'own'), may hold values from -6 to 6
- obs_weight: bfloat16 [64, 2048], P('grp', 'own'), may hold values from 0.25 to 4
- obs_count: int32 [64, 4], P('grp', 'own'), may hold values from 128 to 512, as said below
- dest: int32 [64], replicated, may hold values from 0 to 7, as said below
Outputs:
- analysis: bfloat16 [64, 1024, 512], P('grp', 'own')
Inputs may be any that keep to these rules, and one draw needn't show every extreme that they name: `obs_count`: each entry counts the live leading slots of one owner's block of 512; later slots carry values that must be ignored. The largest entry of every draw equals 512. `dest`: every index of grp is named by exactly 8 groups, and no two groups of one index of grp name the same index.
All inputs are finite; a program needn't handle non-finite values.
Results may differ from a plain program's by a relative error of at most 0.012.
The roundings to bfloat16 on the way count: a program that leaves them out, or rounds other values in their place, can miss the bound.
Values may be sent and summed in bfloat16 or wider, within the bound.
No kernel may reach another device: no remote copies, remote signals or barrier semaphores. Data moves between devices by JAX's collectives and lax.ppermute only.
A program may use at most 128 MiB of HBM per device.

v0:
```python
import jax
import jax.numpy as jnp
from jax import lax
from jax.sharding import PartitionSpec as P

NS_IT = 4


def newton_weights(gram, right_side):
    members = gram.shape[-1]
    eye_mat = jnp.eye(members, dtype=jnp.float32)
    matrix = gram + (members - 1.0) * eye_mat
    norm_scale = jnp.sqrt(jnp.sum(matrix * matrix, axis=(1, 2)))
    root_iter = (matrix / norm_scale[:, None, None]).astype(jnp.bfloat16)
    inverse = jnp.broadcast_to(eye_mat.astype(jnp.bfloat16), matrix.shape)
    for iteration in range(NS_IT):
        product = jnp.einsum("gij,gjk->gik", inverse, root_iter, preferred_element_type=jnp.float32)
        factor = (1.5 * eye_mat - 0.5 * product).astype(jnp.bfloat16)
        root_iter = jnp.einsum(
            "gij,gjk->gik", root_iter, factor, preferred_element_type=jnp.float32
        ).astype(jnp.bfloat16)
        inverse = jnp.einsum(
            "gij,gjk->gik", factor, inverse, preferred_element_type=jnp.float32
        ).astype(jnp.bfloat16)
    inverse_wide = inverse.astype(jnp.float32)
    half_way = jnp.einsum("gij,gj->gi", inverse_wide, right_side, precision=lax.Precision.HIGHEST)
    mean_weight = (
        jnp.einsum("gij,gj->gi", inverse_wide, half_way, precision=lax.Precision.HIGHEST)
        / norm_scale[:, None]
    )
    weights = (
        jnp.sqrt((members - 1.0) / norm_scale)[:, None, None] * inverse_wide
        + mean_weight[:, :, None]
    )
    return weights.astype(jnp.bfloat16)


def solve_weights(obs_pert, weight, source):
    weighted = (obs_pert.astype(jnp.float32) * weight.astype(jnp.float32)[:, :, None]).astype(
        jnp.bfloat16
    )
    gram_local = jnp.einsum("gpk,gpl->gkl", weighted, obs_pert, preferred_element_type=jnp.float32)
    right_local = jnp.einsum("gp,gpk->gk", source, obs_pert, preferred_element_type=jnp.float32)
    gram_part, right_part = (
        lax.psum_scatter(gram_local, "own", scatter_dimension=0, tiled=True),
        lax.psum_scatter(right_local, "own", scatter_dimension=0, tiled=True),
    )
    return lax.all_gather(newton_weights(gram_part, right_part), "own", axis=0, tiled=True)


def apply_weights(state_here, weights):
    state_mean = jnp.mean(state_here.astype(jnp.float32), axis=2, keepdims=True)
    state_pert = (state_here.astype(jnp.float32) - state_mean).astype(jnp.bfloat16)
    result = state_mean + jnp.einsum(
        "grk,gkl->grl", state_pert, weights, preferred_element_type=jnp.float32
    )
    return result.astype(jnp.bfloat16)


def pack_rows(array_in, send_index, send_live):
    picked = jnp.take(array_in, send_index, axis=0)
    keep_mask = send_live.reshape((-1,) + (1,) * (array_in.ndim - 1))
    return jnp.where(keep_mask, picked, jnp.zeros_like(picked))


def body(background, obs_ens, innovation, obs_weight, obs_count, dest):
    grp_size = lax.axis_size("grp")
    grp_index = lax.axis_index("grp")
    local_groups = background.shape[0]
    obs_rows = obs_ens.shape[1]
    obs_mean = jnp.mean(obs_ens.astype(jnp.float32), axis=2, keepdims=True)
    obs_pert = (obs_ens.astype(jnp.float32) - obs_mean).astype(jnp.bfloat16)
    position_in = lax.broadcasted_iota(jnp.int32, (local_groups, obs_rows), 1)
    live_rows = position_in < obs_count
    weight = jnp.where(live_rows, obs_weight, jnp.zeros_like(obs_weight))
    source = (weight.astype(jnp.float32) * innovation.astype(jnp.float32)).astype(jnp.bfloat16)
    group_total = dest.shape[0]
    group_ids = jnp.arange(group_total, dtype=jnp.int32)
    same_dest = dest[None, :] == dest[:, None]
    earlier = group_ids[None, :] < group_ids[:, None]
    arrival_rank = jnp.sum(jnp.where(same_dest & earlier, 1, 0), axis=1).astype(jnp.int32)
    my_dest = lax.dynamic_slice_in_dim(dest, grp_index * local_groups, local_groups)
    peer_ids = jnp.arange(grp_size, dtype=jnp.int32)
    local_ids = jnp.arange(local_groups, dtype=jnp.int32)
    peer_hits = my_dest[None, :] == peer_ids[:, None]
    send_index = jnp.sum(jnp.where(peer_hits, local_ids[None, :], 0), axis=1)
    send_live = jnp.any(peer_hits, axis=1)
    arriving = (dest[None, :] == grp_index) & (arrival_rank[None, :] == local_ids[:, None])
    arrive_group = jnp.sum(jnp.where(arriving, group_ids[None, :], 0), axis=1)
    arrive_source = arrive_group // local_groups
    weights = solve_weights(obs_pert, weight, source)
    result = apply_weights(background, weights)
    return jnp.take(
        lax.all_to_all(
            pack_rows(result, send_index, send_live), "grp", split_axis=0, concat_axis=0, tiled=True
        ),
        arrive_source,
        axis=0,
    )


def solution(mesh):
    return jax.shard_map(
        body,
        mesh=mesh,
        in_specs=(
            P("grp", "own", None),
            P("grp", "own", None),
            P("grp", "own"),
            P("grp", "own"),
            P("grp", "own"),
            P(),
        ),
        out_specs=P("grp", "own", None),
        check_vma=False,
    )
```

profile of v0, /device:TPU:0, one launch (start us, length us, event | category | flops | bytes accessed | tf_op | source)
XLA Modules:
  0.0 316.4 jit_solution(11262889886701384179)
XLA Ops:
  6.5 3.0 convert_reduce_fusion
  9.6 0.4 copy-done
  10.0 6.3 %fusion.1 = f32[8,512,512]{2,1,0:T(8,128)} fusion(f32[8,512]{1,0:T(8,128)S(1)} %fusion.16, bf16[8,512,512]{2,1,0:T(8,128)(2,1)S(1)} %copy-done, f32[8,512]{1,0:T(8,128)S(1)} %broadcast_multiply_fusion), kind=kOutput, calls=%fused_computation.6 | convolution fusion | flops 2166358016 | bytes 12615680 | tf_op jit(solution)/shard_map/gpk,gpl->gkl/dot_general | solution.py:42
  16.4 0.6 copy-done.4
  17.1 2.8 fusion.5
  19.9 0.6 dynamic-slice
  21.1 21.8 %all-reduce = f32[8,512]{1,0:T(8,128)S(1)} all-reduce(f32[8,512]{1,0:T(8,128)S(1)} %bitcast.37), channel_id=3, replica_groups=mesh['grp'=8,'own'=4] {'own'}, use_global_device_ids=true, to_apply=%region_5.6.clone | all-reduce | flops 4096 | bytes 32768
  43.2 121.0 %reduce-scatter.2.cloned.1.call-done = f32[2,512,512]{2,1,0:T(8,128)} async-done(((f32[8,512,512]{2,1,0:T(8,128)}), f32[2,512,512]{2,1,0:T(8,128)}) %reduce-scatter.2.cloned.1.call-update) | async-done | bytes 2097168 | tf_op jit(solution)/shard_map/reduce_scatter | solution.py:45
  164.2 2.1 multiply_reduce_fusion
  166.4 0.6 divide_convert_fusion
  167.0 0.7 subtract_convert_fusion.3
  167.7 0.7 convolution_convert_fusion.5
  168.4 0.7 convolution_convert_fusion.6
  169.1 0.7 subtract_convert_fusion.2
  169.9 0.7 convolution_convert_fusion.3
  170.6 0.7 convolution_convert_fusion.4
  171.3 0.7 subtract_convert_fusion.1
  172.1 1.0 copy-done.8
  173.0 1.7 convolution_convert_fusion.2
  174.7 3.8 %subtract_convert_fusion = bf16[2,512,512]{2,1,0:T(8,128)(2,1)} fusion(bf16[2,512,512]{2,1,0:T(8,128)(2,1)} %convolution_convert_fusion.2, bf16[2,512,512]{2,1,0:T(8,128)(2,1)S(1)} %convolution_convert_fusion.3, bf16[2,512,512]{2,1,0:T(8,128)(2,1)} %copy-done.8, f32[512,512]{1,0:T(8,128)S(1)} %fusion.9), kind=kOutput, calls=%fused_computation.15 | convolution fusion | flops 1075838976 | bytes 5242880 | tf_op jit(solution)/shard_map/gij,gjk->gik/dot_general | solution.py:17
  178.6 2.2 convolution_convert_fusion
  180.8 0.9 fusion.20
  181.7 0.9 fusion.18
  182.7 1.3 add_convert_fusion.1
  184.8 80.8 %all-gather.2.cloned.1.call-done = bf16[8,512,512]{2,1,0:T(8,128)(2,1)} async-done(((bf16[2,512,512]{2,1,0:T(8,128)(2,1)}), bf16[8,512,512]{2,1,0:T(8,128)(2,1)}) %all-gather.2.cloned.1.call-update) | async-done | bytes 4194320 | tf_op jit(solution)/shard_map/all_gather | solution.py:48
  265.6 4.7 %add_convert_fusion = bf16[8,256,512]{2,1,0:T(8,128)(2,1)} fusion(bf16[8,512,512]{2,1,0:T(8,128)(2,1)} %all-gather.2.cloned.1.call-done, bf16[8,256,512]{2,1,0:T(8,128)(2,1)S(1)} %copy-done.2, f32[8,256]{1,0:T(8,128)S(1)} %broadcast_multiply_fusion.1), kind=kOutput, calls=%fused_computation.10 | convolution fusion | flops 1078984704 | bytes 8396800 | tf_op jit(solution)/shard_map/grk,gkl->grl/dot_general | solution.py:54
  270.3 2.3 gather_fusion
  272.6 1.6 select_select_fusion
  274.2 3.7 %all-to-all-start = ((bf16[8,256,512]{2,1,0:T(8,128)(2,1)}), bf16[8,256,512]{2,1,0:T(8,128)(2,1)S(1)}, u32[]{:S(2)}, u32[]{:S(2)}) async-start(bf16[8,256,512]{2,1,0:T(8,128)(2,1)} %select_select_fusion), calls=%async_computation.1 | async-start | bytes 4194304 | tf_op jit(solution)/shard_map/all_to_all | solution.py:94
  278.2 26.3 %all-to-all-done = bf16[8,256,512]{2,1,0:T(8,128)(2,1)S(1)} async-done(((bf16[8,256,512]{2,1,0:T(8,128)(2,1)}), bf16[8,256,512]{2,1,0:T(8,128)(2,1)S(1)}, u32[]{:S(2)}, u32[]{:S(2)}) %all-to-all-start) | async-done | bytes 2097184 | tf_op jit(solution)/shard_map/all_to_all | solution.py:94
  304.4 2.0 gather_fusion.1
  306.4 3.2 %broadcast_select_fusion = bf16[8,256,512]{2,1,0:T(8,128)(2,1)} fusion(bf16[8,256,512]{2,1,0:T(8,128)(2,1)} %gather_fusion.1, pred[8]{0:T(512)(128)(4,1)S(1)} %get-tuple-element.6), kind=kLoop, calls=%fused_computation.22 | loop fusion | flops 1048576 | bytes 4194312 | tf_op jit(solution)/shard_map/jit(_take)/select_n | solution.py:93
  (43 shorter events, 1.7 us)
Async XLA Ops:
  6.5 3.0 copy-start.5
  6.5 3.0 copy-start.3
  6.5 157.6 %reduce-scatter.2.cloned.1.call-start = ((), (), s32[]{:S(2)}) async-start(), calls=%async_computation.2 | async-start | bytes 10485760 | tf_op jit(solution)/shard_map/reduce_scatter | solution.py:45
  6.5 3.5 %copy-start = (bf16[8,512,512]{2,1,0:T(8,128)(2,1)S(1)}, bf16[8,512,512]{2,1,0:T(8,128)(2,1)}, u32[]{:S(2)}) copy-start(bf16[8,512,512]{2,1,0:T(8,128)(2,1)} %param.9) | copy-start | bytes 12582916
  16.3 0.7 copy-start.4
  16.3 249.2 %all-gather.2.cloned.1.call-start = ((), (), s32[]{:S(2)}) async-start(), calls=%async_computation.3 | async-start | bytes 5242880 | tf_op jit(solution)/shard_map/all_gather | solution.py:48
  17.1 2.8 copy-start.7
  164.2 2.2 copy-start.1
  172.0 1.0 copy-start.8
  181.7 2.3 copy-start.6
  181.7 2.7 copy-start.2
  274.2 30.3 %all-to-all-start = ((bf16[8,256,512]{2,1,0:T(8,128)(2,1)}), bf16[8,256,512]{2,1,0:T(8,128)(2,1)S(1)}, u32[]{:S(2)}, u32[]{:S(2)}) async-start(bf16[8,256,512]{2,1,0:T(8,128)(2,1)} %select_select_fusion), calls=%async_computation.1 | async-start | bytes 4194304 | tf_op jit(solution)/shard_map/all_to_all | solution.py:94
Sparse Core Ops, SparseCore 0:
  16.4 147.6 reduce-scatter.1
  184.2 81.3 all-gather.1
where the time goes:
time: 317 us; the launch traced here: 316 us
  waiting for transfers between devices  228 us (72%)
  matrix products  28.4 us (9%)
  blocking collectives  21.8 us (7%)
  between operations  14.3 us (5%)
  other arithmetic  13.2 us (4%)
  local copies, waits for them, and re-layouts  7.05 us (2%)
  starting transfers between devices  3.7 us (1%)
    reduce_scatter x1, waiting for transfers between devices, solve_weights(): lax.psum_scatter(gram_local, 'own', scatter_dimension=0, tiled=True)  121 us
    all_gather x1, waiting for transfers between devices, solve_weights(): lax.all_gather(newton_weights(gram_part, right_part), 'own', axis=0, tile...  80.8 us
    all_to_all x1, waiting for transfers between devices, body(): lax.all_to_all(pack_rows(result, send_index, send_live), 'grp', split_axi...  26.3 us
    unnamed x1, blocking collectives  21.8 us
  transfers between devices with their start and end apart: 3, of which 3 were waited for; matrix products, arithmetic and copies ran while one was open for 1% of the time, Pallas kernels for 0%

commit v1 on v0

v1 whole, which is shorter than its diff:
```python
import functools

import jax
import jax.numpy as jnp
from jax import lax
from jax.experimental import pallas as pl
from jax.experimental.pallas import tpu as pltpu
from jax.sharding import PartitionSpec as P

NS_IT = 4
LANES = 128
EXTRA = 16
F32 = jnp.float32
BF16 = jnp.bfloat16


def block_pairs(blocks):
    return [(i, j) for i in range(blocks) for j in range(i + 1, blocks)]


def packed_rows(members):
    blocks = members // LANES
    return (len(block_pairs(blocks)) + blocks // 2) * LANES + EXTRA


def square_iota():
    row = lax.broadcasted_iota(jnp.int32, (LANES, LANES), 0)
    col = lax.broadcasted_iota(jnp.int32, (LANES, LANES), 1)
    return row, col


def gram_kernel(offset, order_ref, count_ref, obs_ref, weight_ref, innov_ref, out_ref):
    group = order_ref[offset + pl.program_id(0)]
    slots, members = obs_ref.shape[1:]
    blocks = members // LANES
    obs = obs_ref[0].astype(F32)
    mean = jnp.mean(obs, axis=1, keepdims=True)
    pert = (obs - mean).astype(BF16)

    def own_row(ref):
        rows = lax.broadcasted_iota(jnp.int32, ref.shape, 0)
        return jnp.sum(jnp.where(rows == group, ref[...].astype(F32), 0.0), axis=0, keepdims=True)

    live = lax.broadcasted_iota(jnp.int32, (1, slots), 1) < count_ref[group]
    weight = jnp.where(live, own_row(weight_ref), 0.0)
    source = (weight * own_row(innov_ref)).astype(BF16)
    column = jnp.transpose(jnp.broadcast_to(weight, (LANES, slots)))
    column = jnp.concatenate([column] * blocks, axis=1)
    weighted = (pert.astype(F32) * column).astype(BF16)

    rhs = jnp.dot(jnp.broadcast_to(source, (16, slots)), pert, preferred_element_type=F32)[:8]
    parts = {}
    for i in range(0, blocks, 2):
        strip = lax.dot_general(
            weighted[:, i * LANES:(i + 2) * LANES], pert[:, i * LANES:],
            (((0,), (0,)), ((), ())), preferred_element_type=F32)
        for a in range(2):
            for j in range(i + a, blocks):
                parts[i + a, j] = strip[a * LANES:(a + 1) * LANES, (j - i) * LANES:(j - i + 1) * LANES]
    row, col = square_iota()
    at = 0
    for i, j in block_pairs(blocks):
        out_ref[0, at:at + LANES] = parts[i, j].astype(BF16)
        at += LANES
    sub = lax.broadcasted_iota(jnp.int32, (8, LANES), 0)
    diag = jnp.zeros((8, LANES), F32)
    for i in range(0, blocks, 2):
        out_ref[0, at:at + LANES] = jnp.where(row <= col, parts[i, i], parts[i + 1, i + 1]).astype(BF16)
        at += LANES
        line = jnp.sum(jnp.where(row == col, parts[i + 1, i + 1], 0.0), axis=0, keepdims=True)
        diag = jnp.where(sub == i // 2, line, diag)
    half = 4
    wide = jnp.zeros((8, LANES), F32)
    for k in range(blocks):
        wide = jnp.where(sub % half == k, rhs[:, k * LANES:(k + 1) * LANES], wide)
    high = wide.astype(BF16).astype(F32)
    wide = jnp.where(sub < half, high, wide - high)
    out_ref[0, at:at + EXTRA] = jnp.concatenate([wide, diag], axis=0).astype(BF16)


def gram_call(obs_ens, weight, innov, order, count, offset, number):
    groups, slots, members = obs_ens.shape
    rows = packed_rows(members)
    return pl.pallas_call(
        functools.partial(gram_kernel, offset),
        out_shape=jax.ShapeDtypeStruct((number, rows, LANES), BF16),
        grid_spec=pltpu.PrefetchScalarGridSpec(
            num_scalar_prefetch=2,
            grid=(number,),
            in_specs=[
                pl.BlockSpec((1, slots, members), lambda i, order, count: (order[offset + i], 0, 0)),
                pl.BlockSpec((groups, slots), lambda i, order, count: (0, 0)),
                pl.BlockSpec((groups, slots), lambda i, order, count: (0, 0)),
            ],
            out_specs=pl.BlockSpec((1, rows, LANES), lambda i, order, count: (i, 0, 0)),
        ),
        cost_estimate=pl.CostEstimate(
            flops=2 * number * slots * members * members, transcendentals=0,
            bytes_accessed=number * 2 * (slots * members + rows * LANES)),
        name="gram",
    )(order, count, obs_ens, weight, innov)


def add_kernel(a_ref, b_ref, out_ref):
    total = a_ref[0].astype(F32) + b_ref[0].astype(F32)
    rows = total.shape[0] - EXTRA
    out_ref[0, :rows] = total[:rows].astype(BF16)
    tail = total[rows:]
    sub = lax.broadcasted_iota(jnp.int32, (8, LANES), 0)
    wide = tail[:8] + pltpu.roll(tail[:8], 4, 0)
    high = wide.astype(BF16).astype(F32)
    wide = jnp.where(sub < 4, high, wide - high)
    out_ref[0, rows:] = jnp.concatenate([wide, tail[8:]], axis=0).astype(BF16)


def add_call(a, b):
    number, rows, lanes = a.shape
    spec = pl.BlockSpec((1, rows, lanes), lambda i: (i, 0, 0))
    return pl.pallas_call(
        add_kernel,
        out_shape=jax.ShapeDtypeStruct(a.shape, a.dtype),
        grid=(number,), in_specs=[spec, spec], out_specs=spec,
        cost_estimate=pl.CostEstimate(flops=a.size, transcendentals=0, bytes_accessed=6 * a.size),
        name="add_parts",
    )(a, b)


def solve_kernel(order_ref, total_ref, state_ref, out_ref):
    members = state_ref.shape[2]
    blocks = members // LANES
    row, col = square_iota()
    grid = {}
    at = 0
    for i, j in block_pairs(blocks):
        part = total_ref[0, at:at + LANES].astype(F32)
        grid[i, j] = part
        grid[j, i] = jnp.transpose(part)
        at += LANES
    base = at + (blocks // 2) * LANES
    tail = total_ref[0, base:base + EXTRA].astype(F32)
    for i in range(0, blocks, 2):
        part = total_ref[0, at:at + LANES].astype(F32)
        flip = jnp.transpose(part)
        at += LANES
        grid[i, i] = jnp.where(row <= col, part, flip)
        low = jnp.where(row > col, part, flip)
        line = tail[8 + i // 2:9 + i // 2]
        grid[i + 1, i + 1] = jnp.where(row == col, line, low)
    gram = jnp.concatenate(
        [jnp.concatenate([grid[i, j] for j in range(blocks)], axis=1) for i in range(blocks)], axis=0)
    big_row = lax.broadcasted_iota(jnp.int32, (members, members), 0)
    big_col = lax.broadcasted_iota(jnp.int32, (members, members), 1)
    eye = big_row == big_col
    matrix = gram + jnp.where(eye, members - 1.0, 0.0)
    square = jnp.sum(matrix * matrix, axis=0, keepdims=True)
    scale = jnp.sqrt(jnp.sum(square, axis=1, keepdims=True))
    root = (matrix / scale).astype(BF16)

    def mul(a, b):
        return jnp.dot(a, b, preferred_element_type=F32)

    inverse = None
    for iteration in range(NS_IT):
        product = root.astype(F32) if inverse is None else mul(inverse, root)
        factor = (jnp.where(eye, 1.5, 0.0) - 0.5 * product).astype(BF16)
        inverse = factor if inverse is None else mul(factor, inverse).astype(BF16)
        if iteration + 1 < NS_IT:
            root = mul(root, factor).astype(BF16)

    sub = lax.broadcasted_iota(jnp.int32, (16, LANES), 0)
    lines = [
        jnp.where(sub == 0, tail[k:k + 1], jnp.where(sub == 1, tail[4 + k:5 + k], 0.0))
        for k in range(blocks)]
    rhs = jnp.concatenate(lines, axis=1).astype(BF16)
    half_way = jnp.sum(mul(rhs, inverse), axis=0, keepdims=True)
    wide = inverse.astype(F32)
    mean_weight = jnp.sum(wide * half_way, axis=1, keepdims=True) / scale
    weights = (jnp.sqrt((members - 1.0) / scale) * wide + mean_weight).astype(BF16)

    state = state_ref[0].astype(F32)
    state_mean = jnp.mean(state, axis=1, keepdims=True)
    state_pert = (state - state_mean).astype(BF16)
    out_ref[0] = (state_mean + mul(state_pert, weights)).astype(BF16)


def solve_call(total, background, order, offset):
    number, rows, lanes = total.shape
    here, members = background.shape[1:]
    return pl.pallas_call(
        solve_kernel,
        out_shape=jax.ShapeDtypeStruct((number, here, members), BF16),
        grid_spec=pltpu.PrefetchScalarGridSpec(
            num_scalar_prefetch=1,
            grid=(number,),
            in_specs=[
                pl.BlockSpec((1, rows, lanes), lambda i, order: (i, 0, 0)),
                pl.BlockSpec((1, here, members), lambda i, order: (order[offset + i], 0, 0)),
            ],
            out_specs=pl.BlockSpec((1, here, members), lambda i, order: (i, 0, 0)),
        ),
        cost_estimate=pl.CostEstimate(
            flops=number * (3 * NS_IT - 3) * 2 * members ** 3, transcendentals=0,
            bytes_accessed=number * (2 * rows * lanes + 4 * here * members)),
        name="solve",
    )(order, total, background)


def pack_rows(array_in, send_index, send_live):
    picked = jnp.take(array_in, send_index, axis=0)
    keep_mask = send_live.reshape((-1,) + (1,) * (array_in.ndim - 1))
    return jnp.where(keep_mask, picked, jnp.zeros_like(picked))


def send_all(result, dest, my_dest, grp_size, grp_index):
    local_groups = result.shape[0]
    group_ids = jnp.arange(dest.shape[0], dtype=jnp.int32)
    same_dest = dest[None, :] == dest[:, None]
    earlier = group_ids[None, :] < group_ids[:, None]
    arrival_rank = jnp.sum(jnp.where(same_dest & earlier, 1, 0), axis=1).astype(jnp.int32)
    peer_ids = jnp.arange(grp_size, dtype=jnp.int32)
    local_ids = jnp.arange(local_groups, dtype=jnp.int32)
    peer_hits = my_dest[None, :] == peer_ids[:, None]
    send_index = jnp.sum(jnp.where(peer_hits, local_ids[None, :], 0), axis=1)
    send_live = jnp.any(peer_hits, axis=1)
    arriving = (dest[None, :] == grp_index) & (arrival_rank[None, :] == local_ids[:, None])
    arrive_group = jnp.sum(jnp.where(arriving, group_ids[None, :], 0), axis=1)
    received = lax.all_to_all(
        pack_rows(result, send_index, send_live), "grp", split_axis=0, concat_axis=0, tiled=True)
    return jnp.take(received, arrive_group // local_groups, axis=0)


def body(background, obs_ens, innovation, obs_weight, obs_count, dest):
    grp_size, own_size = lax.axis_size("grp"), lax.axis_size("own")
    grp_index, own_index = lax.axis_index("grp"), lax.axis_index("own")
    groups = background.shape[0]
    my_dest = lax.dynamic_slice_in_dim(dest, grp_index * groups, groups)
    odd = own_index % 2
    run = groups // 4
    far = list(range(groups - 1, -1, -1))
    head, last = far[:2 * run], far[2 * run:]
    runs = [head[:run], head[run:], last[1::2], last[0::2]]
    runs[2], runs[3] = sorted(runs[2], reverse=True), sorted(runs[3], reverse=True)
    even_seq = runs[0] + runs[1] + runs[2] + runs[3]
    odd_seq = runs[1] + runs[0] + runs[3] + runs[2]
    distance = jnp.where(odd == 1, jnp.array(odd_seq, jnp.int32), jnp.array(even_seq, jnp.int32))
    direct = grp_size == groups and groups & (groups - 1) == 0
    if direct:
        target = grp_index ^ distance
        order = jnp.sum(
            jnp.where(my_dest[None, :] == target[:, None], jnp.arange(groups, dtype=jnp.int32)[None, :], 0),
            axis=1).astype(jnp.int32)
    else:
        order = distance
    count = obs_count[:, 0]

    pair = [(i, i ^ 1) for i in range(own_size)]
    crosses = []
    while 2 << len(crosses) < own_size:
        step = 2 << len(crosses)
        crosses.append([(i, i ^ step) for i in range(own_size)])
    results = []
    for chunk in range(2):
        at = 2 * run * chunk
        send = gram_call(obs_ens, obs_weight, innovation, order, count, at + run, run)
        keep = gram_call(obs_ens, obs_weight, innovation, order, count, at, run)
        mine = add_call(keep, lax.ppermute(send, "own", pair))
        for cross in crosses:
            mine = add_call(mine, lax.ppermute(mine, "own", cross))
        other = lax.ppermute(mine, "own", pair)
        for total, offset in ((mine, at), (other, at + run)):
            done = solve_call(total, background, order, offset)
            results += [done[k:k + 1] for k in range(run)]
    if not direct:
        back = jnp.zeros_like(order).at[order].set(jnp.arange(groups, dtype=jnp.int32))
        result = jnp.take(jnp.concatenate(results, axis=0), back, axis=0)
        return send_all(result, dest, my_dest, grp_size, grp_index)
    out = jnp.zeros(background.shape, background.dtype)
    for slot, done in enumerate(results):
        pairs = []
        for i in range(grp_size):
            for o in range(own_size):
                step = (odd_seq if o % 2 else even_seq)[slot]
                pairs.append((i * own_size + o, (i ^ step) * own_size + o))
        arrived = lax.ppermute(done, ("grp", "own"), pairs)
        out = lax.dynamic_update_slice_in_dim(out, arrived, target[slot], 0)
    return out


def solution(mesh):
    return jax.shard_map(
        body,
        mesh=mesh,
        in_specs=(
            P("grp", "own", None),
            P("grp", "own", None),
            P("grp", "own"),
            P("grp", "own"),
            P("grp", "own"),
            P(),
        ),
        out_specs=P("grp", "own", None),
        check_vma=False,
    )
```

time: 317 us -> 136 us (0.43)
  waiting for transfers between devices: 228 us -> 12.5 us
  Pallas kernels: 0 us -> 64.1 us
  matrix products: 28.4 us -> 0 us
  starting transfers between devices: 3.7 us -> 28.4 us
  blocking collectives: 21.8 us -> 0 us
  other arithmetic: 13.2 us -> 1.36 us
  local copies, waits for them, and re-layouts: 7.05 us -> 14.4 us
    reduce_scatter x1 -> x0, waiting for transfers between devices: 121 us -> none  [solve_weights(): lax.psum_scatter(gram_local, 'own', scatter_dimension=0, tiled=True)]
    all_gather x1 -> x0, waiting for transfers between devices: 80.8 us -> none  [solve_weights(): lax.all_gather(newton_weights(gram_part, right_part), 'own', axis=0, tile...]
    pallas_call x0 -> x12, Pallas kernels: none -> 64.1 us  [the longest x4 41.1 us: solve_call(): pl.pallas_call(solve_kernel, out_shape=jax.ShapeDtypeStruct((number, here...]
    dot_general x15 -> x0, matrix products: 28.4 us -> none  [the longest x1 6.28 us: solve_weights(): jnp.einsum('gpk,gpl->gkl', weighted, obs_pert, preferred_element_type=jnp...]
    ppermute x0 -> x14, starting transfers between devices: none -> 28.4 us  [the longest x2 11.5 us: body(): other = lax.ppermute(mine, 'own', pair)]
    all_to_all x1 -> x0, waiting for transfers between devices: 26.3 us -> none  [body(): lax.all_to_all(pack_rows(result, send_index, send_live), 'grp', split_axi...]
    unnamed x1 -> x0, blocking collectives: 21.8 us -> none
    ppermute x0 -> x14, waiting for transfers between devices: none -> 12.5 us  [the longest x8 6.87 us: body(): arrived = lax.ppermute(done, ('grp', 'own'), pairs)]
  transfers between devices with their start and end apart: 3 -> 14, of which waited for: 3 -> 3; matrix products, arithmetic and copies ran while one was open for 1% -> 6% of each run, Pallas kernels for 0% -> 44%
where the time goes in v1:
time: 136 us
  Pallas kernels  64.1 us (47%)
  starting transfers between devices  28.4 us (21%)
  between operations  14.8 us (11%)
  local copies, waits for them, and re-layouts  14.4 us (11%)
  waiting for transfers between devices  12.5 us (9%)
  other arithmetic  1.36 us (1%)
    pallas_call x4, Pallas kernels, solve_call(): pl.pallas_call(solve_kernel, out_shape=jax.ShapeDtypeStruct((number, here...  41.1 us
    pallas_call x4, Pallas kernels, gram_call(): pl.pallas_call(functools.partial(gram_kernel, offset), out_shape=jax.Shap...  15.1 us
    ppermute x2, starting transfers between devices, body(): other = lax.ppermute(mine, 'own', pair)  11.5 us
    ppermute x8, starting transfers between devices, body(): arrived = lax.ppermute(done, ('grp', 'own'), pairs)  10.8 us
    pallas_call x4, Pallas kernels, add_call(): pl.pallas_call(add_kernel, out_shape=jax.ShapeDtypeStruct(a.shape, a.dtyp...  7.85 us
    ppermute x8, waiting for transfers between devices, body(): arrived = lax.ppermute(done, ('grp', 'own'), pairs)  6.87 us
    slice x4, local copies, waits for them, and re-layouts, body(): results += [done[k:k + 1] for k in range(run)]  6.56 us
    ppermute x2, waiting for transfers between devices, body(): mine = add_call(keep, lax.ppermute(send, 'own', pair))  5.59 us
  transfers between devices with their start and end apart: 14, of which 3 were waited for; matrix products, arithmetic and copies ran while one was open for 6% of the time, Pallas kernels for 44%

profile of v1, /device:TPU:0, one launch (start us, length us, event | category | flops | bytes accessed | tf_op | source)
XLA Modules:
  0.0 135.6 jit_solution(2002627245822785756)
XLA Ops:
  2.1 3.8 %gram.5 = bf16[2,1040,128]{2,1,0:T(8,128)(2,1)} custom-call(s32[8]{0:T(128)} %select_reduce_fusion.order_ref, s32[8]{0:T(128)} %bitcast.9, bf16[8,512,512]{2,1,0:T(8,128)(2,1)} %obs_ref.7, bf16[8,512]{1,0:T(8,128)(2,1)} %weight_ref.7, bf16[8,512]{1,0:T(8,128)(2,1)} %innov_ref.7), custom_call_target="tpu_custom_call" | custom-call | flops 536870912 | bytes 1581056 | tf_op jit(solution)/shard_map/gram/pallas_call | solution.py:84
  5.9 3.1 %collective-permute-start = (bf16[2,1040,128]{2,1,0:T(8,128)(2,1)}, bf16[2,1040,128]{2,1,0:T(8,128)(2,1)S(1)}, u32[]{:S(2)}, u32[]{:S(2)}) collective-permute-start(bf16[2,1040,128]{2,1,0:T(8,128)(2,1)} %gram.5), channel_id=1, source_target_pairs={{0,1},{1,0},{2,3},{3,2},{4,5},{5,4},{6,7},{7,6},{8,9},{9,8},{10,11... | collective-permute-start | bytes 1597448 | tf_op jit(solution)/shard_map/ppermute | solution.py:266
  8.9 3.8 %gram.7 = bf16[2,1040,128]{2,1,0:T(8,128)(2,1)} custom-call(s32[8]{0:T(128)} %select_reduce_fusion.order_ref, s32[8]{0:T(128)} %bitcast.10, bf16[8,512,512]{2,1,0:T(8,128)(2,1)} %obs_ref.7, bf16[8,512]{1,0:T(8,128)(2,1)} %weight_ref.7, bf16[8,512]{1,0:T(8,128)(2,1)} %innov_ref.7), custom_call_target="tpu_custom_call" | custom-call | flops 536870912 | bytes 1581056 | tf_op jit(solution)/shard_map/gram/pallas_call | solution.py:84
  12.7 3.8 %gram.4.a_ref = bf16[2,1040,128]{2,1,0:T(8,128)(2,1)} custom-call(s32[8]{0:T(128)} %select_reduce_fusion.order_ref, s32[8]{0:T(128)} %bitcast.11, bf16[8,512,512]{2,1,0:T(8,128)(2,1)} %obs_ref.7, bf16[8,512]{1,0:T(8,128)(2,1)} %weight_ref.7, bf16[8,512]{1,0:T(8,128)(2,1)} %innov_ref.7), custom_call_target="tpu_custom_call" | custom-call | flops 536870912 | bytes 1581056 | tf_op jit(solution)/shard_map/gram/pallas_call | solution.py:84
  16.5 5.6 %collective-permute-done.b_ref = bf16[2,1040,128]{2,1,0:T(8,128)(2,1)S(1)} collective-permute-done((bf16[2,1040,128]{2,1,0:T(8,128)(2,1)}, bf16[2,1040,128]{2,1,0:T(8,128)(2,1)S(1)}, u32[]{:S(2)}, u32[]{:S(2)}) %collective-permute-start) | collective-permute-done | bytes 532512 | tf_op jit(solution)/shard_map/ppermute | solution.py:266
  22.9 2.0 %add_parts.4.a_ref = bf16[2,1040,128]{2,1,0:T(8,128)(2,1)} custom-call(bf16[2,1040,128]{2,1,0:T(8,128)(2,1)} %gram.4.a_ref, bf16[2,1040,128]{2,1,0:T(8,128)(2,1)} %copy-done.5), custom_call_target="tpu_custom_call" | custom-call | flops 266240 | bytes 1597440 | tf_op jit(solution)/shard_map/add_parts/pallas_call | solution.py:119
  24.8 3.0 %collective-permute-start.1 = (bf16[2,1040,128]{2,1,0:T(8,128)(2,1)}, bf16[2,1040,128]{2,1,0:T(8,128)(2,1)S(1)}, u32[]{:S(2)}, u32[]{:S(2)}) collective-permute-start(bf16[2,1040,128]{2,1,0:T(8,128)(2,1)} %add_parts.4.a_ref), channel_id=1, source_target_pairs={{0,2},{1,3},{2,0},{3,1},{4,6},{5,7},{6,4},{7,5},{8,10},{9,11},{10,... | collective-permute-start | bytes 1597448 | tf_op jit(solution)/shard_map/ppermute | solution.py:268
  43.2 3.8 %gram.6.a_ref = bf16[2,1040,128]{2,1,0:T(8,128)(2,1)} custom-call(s32[8]{0:T(128)} %select_reduce_fusion.order_ref, s32[8]{0:T(128)} %bitcast.12, bf16[8,512,512]{2,1,0:T(8,128)(2,1)} %obs_ref.7, bf16[8,512]{1,0:T(8,128)(2,1)} %weight_ref.7, bf16[8,512]{1,0:T(8,128)(2,1)} %innov_ref.7), custom_call_target="tpu_custom_call" | custom-call | flops 536870912 | bytes 1581056 | tf_op jit(solution)/shard_map/gram/pallas_call | solution.py:84
  47.0 0.8 copy-done.1
  47.8 2.0 %add_parts.6.a_ref = bf16[2,1040,128]{2,1,0:T(8,128)(2,1)} custom-call(bf16[2,1040,128]{2,1,0:T(8,128)(2,1)} %gram.6.a_ref, bf16[2,1040,128]{2,1,0:T(8,128)(2,1)} %copy-done.1), custom_call_target="tpu_custom_call" | custom-call | flops 266240 | bytes 1597440 | tf_op jit(solution)/shard_map/add_parts/pallas_call | solution.py:119
  49.8 0.8 copy-done.2
  50.6 2.0 %add_parts.5.total_ref = bf16[2,1040,128]{2,1,0:T(8,128)(2,1)} custom-call(bf16[2,1040,128]{2,1,0:T(8,128)(2,1)} %add_parts.4.a_ref, bf16[2,1040,128]{2,1,0:T(8,128)(2,1)} %copy-done.2), custom_call_target="tpu_custom_call" | custom-call | flops 266240 | bytes 1597440 | tf_op jit(solution)/shard_map/add_parts/pallas_call | solution.py:119
  52.6 11.5 %collective-permute-start.4 = (bf16[2,1040,128]{2,1,0:T(8,128)(2,1)}, bf16[2,1040,128]{2,1,0:T(8,128)(2,1)}, u32[]{:S(2)}, u32[]{:S(2)}) collective-permute-start(bf16[2,1040,128]{2,1,0:T(8,128)(2,1)} %add_parts.5.total_ref), channel_id=1, source_target_pairs={{0,1},{1,0},{2,3},{3,2},{4,5},{5,4},{6,7},{7,6},{8,9},{9,8},{10,11... | collective-permute-start | bytes 1597448 | tf_op jit(solution)/shard_map/ppermute | solution.py:269
  64.1 10.2 %solve.4 = bf16[2,256,512]{2,1,0:T(8,128)(2,1)} custom-call(s32[8]{0:T(128)} %select_reduce_fusion.order_ref, bf16[2,1040,128]{2,1,0:T(8,128)(2,1)} %add_parts.5.total_ref, bf16[8,256,512]{2,1,0:T(8,128)(2,1)} %state_ref.7), custom_call_target="tpu_custom_call" | custom-call | flops 4831838208 | bytes 1581056 | tf_op jit(solution)/shard_map/solve/pallas_call | solution.py:189
  74.3 1.8 %fusion.4 = (bf16[1,256,512]{2,1,0:T(8,128)(2,1)}, bf16[1,256,512]{2,1,0:T(8,128)(2,1)S(1)}) fusion(bf16[2,256,512]{2,1,0:T(8,128)(2,1)} %solve.4), kind=kLoop, calls=%fused_computation.14 | loop fusion | bytes 1048576 | tf_op jit(solution)/shard_map/slice | solution.py:272
  76.1 0.8 copy-done.4
  76.9 2.0 %add_parts.7.total_ref = bf16[2,1040,128]{2,1,0:T(8,128)(2,1)} custom-call(bf16[2,1040,128]{2,1,0:T(8,128)(2,1)} %add_parts.6.a_ref, bf16[2,1040,128]{2,1,0:T(8,128)(2,1)} %copy-done.4), custom_call_target="tpu_custom_call" | custom-call | flops 266240 | bytes 1597440 | tf_op jit(solution)/shard_map/add_parts/pallas_call | solution.py:119
  78.8 10.4 %solve.6 = bf16[2,256,512]{2,1,0:T(8,128)(2,1)} custom-call(s32[8]{0:T(128)} %select_reduce_fusion.order_ref, bf16[2,1040,128]{2,1,0:T(8,128)(2,1)} %add_parts.7.total_ref, bf16[8,256,512]{2,1,0:T(8,128)(2,1)} %state_ref.7), custom_call_target="tpu_custom_call" | custom-call | flops 4831838208 | bytes 1581056 | tf_op jit(solution)/shard_map/solve/pallas_call | solution.py:189
  89.2 2.2 %collective-permute-start.3 = (bf16[1,256,512]{2,1,0:T(8,128)(2,1)}, bf16[1,256,512]{2,1,0:T(8,128)(2,1)S(1)}, u32[]{:S(2)}, u32[]{:S(2)}) collective-permute-start(bf16[1,256,512]{2,1,0:T(8,128)(2,1)} %get-tuple-element.11), channel_id=1, source_target_pairs={{0,24},{1,17},{2,26},{3,19},{4,28},{5,21},{6,30},{7,23},{8,16},{9,... | collective-permute-start | bytes 786440 | tf_op jit(solution)/shard_map/ppermute | solution.py:284
  91.4 1.9 %fusion.2 = (bf16[1,256,512]{2,1,0:T(8,128)(2,1)}, bf16[1,256,512]{2,1,0:T(8,128)(2,1)}) fusion(bf16[2,256,512]{2,1,0:T(8,128)(2,1)} %solve.6), kind=kLoop, calls=%fused_computation.12 | loop fusion | bytes 1048576 | tf_op jit(solution)/shard_map/slice | solution.py:272
  93.8 1.6 %collective-permute-start.10 = (bf16[1,256,512]{2,1,0:T(8,128)(2,1)}, bf16[1,256,512]{2,1,0:T(8,128)(2,1)S(1)}, u32[]{:S(2)}, u32[]{:S(2)}) collective-permute-start(bf16[1,256,512]{2,1,0:T(8,128)(2,1)} %get-tuple-element.7), channel_id=1, source_target_pairs={{0,0},{1,5},{2,2},{3,7},{4,4},{5,1},{6,6},{7,3},{8,8},{9,13},{10,1... | collective-permute-start | bytes 786440 | tf_op jit(solution)/shard_map/ppermute | solution.py:284
  95.6 2.8 %collective-permute-done.3 = bf16[1,256,512]{2,1,0:T(8,128)(2,1)S(1)} collective-permute-done((bf16[1,256,512]{2,1,0:T(8,128)(2,1)}, bf16[1,256,512]{2,1,0:T(8,128)(2,1)S(1)}, u32[]{:S(2)}, u32[]{:S(2)}) %collective-permute-start.3) | collective-permute-done | bytes 262176 | tf_op jit(solution)/shard_map/ppermute | solution.py:284
  98.5 10.2 %solve.5 = bf16[2,256,512]{2,1,0:T(8,128)(2,1)} custom-call(s32[8]{0:T(128)} %select_reduce_fusion.order_ref, bf16[2,1040,128]{2,1,0:T(8,128)(2,1)} %collective-permute-done.4.total_ref, bf16[8,256,512]{2,1,0:T(8,128)(2,1)} %state_ref.7), custom_call_target="tpu_custom_call" | custom-call | flops 4831838208 | bytes 1581056 | tf_op jit(solution)/shard_map/solve/pallas_call | solution.py:189
  108.7 1.9 %fusion.3 = (bf16[1,256,512]{2,1,0:T(8,128)(2,1)}, bf16[1,256,512]{2,1,0:T(8,128)(2,1)}) fusion(bf16[2,256,512]{2,1,0:T(8,128)(2,1)} %solve.5), kind=kLoop, calls=%fused_computation.13 | loop fusion | bytes 1048576 | tf_op jit(solution)/shard_map/slice | solution.py:272
  110.6 2.3 %collective-permute-start.5 = (bf16[1,256,512]{2,1,0:T(8,128)(2,1)}, bf16[1,256,512]{2,1,0:T(8,128)(2,1)}, u32[]{:S(2)}, u32[]{:S(2)}) collective-permute-start(bf16[1,256,512]{2,1,0:T(8,128)(2,1)} %get-tuple-element.10), channel_id=1, source_target_pairs={{0,20},{1,29},{2,22},{3,31},{4,16},{5,25},{6,18},{7,27},{8,28},{9,... | collective-permute-start | bytes 786440 | tf_op jit(solution)/shard_map/ppermute | solution.py:284
  112.9 1.6 %collective-permute-start.6 = (bf16[1,256,512]{2,1,0:T(8,128)(2,1)}, bf16[1,256,512]{2,1,0:T(8,128)(2,1)S(1)}, u32[]{:S(2)}, u32[]{:S(2)}) collective-permute-start(bf16[1,256,512]{2,1,0:T(8,128)(2,1)} %get-tuple-element.9), channel_id=1, source_target_pairs={{0,16},{1,25},{2,18},{3,27},{4,20},{5,29},{6,22},{7,31},{8,24},{9,... | collective-permute-start | bytes 786440 | tf_op jit(solution)/shard_map/ppermute | solution.py:284
  114.5 10.2 %solve.7 = bf16[2,256,512]{2,1,0:T(8,128)(2,1)} custom-call(s32[8]{0:T(128)} %select_reduce_fusion.order_ref, bf16[2,1040,128]{2,1,0:T(8,128)(2,1)} %collective-permute-done.11.total_ref, bf16[8,256,512]{2,1,0:T(8,128)(2,1)} %state_ref.7), custom_call_target="tpu_custom_call" | custom-call | flops 4831838208 | bytes 1581056 | tf_op jit(solution)/shard_map/solve/pallas_call | solution.py:189
  124.7 1.1 fusion.1
  125.9 2.5 %collective-permute-start.13 = (bf16[1,256,512]{2,1,0:T(8,128)(2,1)S(1)}, bf16[1,256,512]{2,1,0:T(8,128)(2,1)S(1)}, u32[]{:S(2)}, u32[]{:S(2)}) collective-permute-start(bf16[1,256,512]{2,1,0:T(8,128)(2,1)S(1)} %get-tuple-element.5), channel_id=1, source_target_pairs={{0,4},{1,1},{2,6},{3,3},{4,0},{5,5},{6,2},{7,7},{8,12},{9,9},{10,1... | collective-permute-start | bytes 786440 | tf_op jit(solution)/shard_map/ppermute | solution.py:284
  128.4 1.0 constant_dynamic-update-slice_fusion.4
  129.5 4.0 %collective-permute-done.12 = bf16[1,256,512]{2,1,0:T(8,128)(2,1)S(1)} collective-permute-done((bf16[1,256,512]{2,1,0:T(8,128)(2,1)S(1)}, bf16[1,256,512]{2,1,0:T(8,128)(2,1)S(1)}, u32[]{:S(2)}, u32[]{:S(2)}) %collective-permute-start.12) | collective-permute-done | bytes 262176 | tf_op jit(solution)/shard_map/ppermute | solution.py:284
  133.6 1.3 copy-done
  (37 shorter events, 5.2 us)
Async XLA Ops:
  5.9 16.2 %collective-permute-start = (bf16[2,1040,128]{2,1,0:T(8,128)(2,1)}, bf16[2,1040,128]{2,1,0:T(8,128)(2,1)S(1)}, u32[]{:S(2)}, u32[]{:S(2)}) collective-permute-start(bf16[2,1040,128]{2,1,0:T(8,128)(2,1)} %gram.5), channel_id=1, source_target_pairs={{0,1},{1,0},{2,3},{3,2},{4,5},{5,4},{6,7},{7,6},{8,9},{9,8},{10,11... | collective-permute-start | bytes 1597448 | tf_op jit(solution)/shard_map/ppermute | solution.py:266
  12.7 34.3 %collective-permute-start.7 = (bf16[2,1040,128]{2,1,0:T(8,128)(2,1)}, bf16[2,1040,128]{2,1,0:T(8,128)(2,1)S(1)}, u32[]{:S(2)}, u32[]{:S(2)}) collective-permute-start(bf16[2,1040,128]{2,1,0:T(8,128)(2,1)} %gram.7), channel_id=1, source_target_pairs={{0,1},{1,0},{2,3},{3,2},{4,5},{5,4},{6,7},{7,6},{8,9},{9,8},{10,11... | collective-permute-start | bytes 1597448 | tf_op jit(solution)/shard_map/ppermute | solution.py:266
  22.1 0.8 copy-start.5
  24.8 25.0 %collective-permute-start.1 = (bf16[2,1040,128]{2,1,0:T(8,128)(2,1)}, bf16[2,1040,128]{2,1,0:T(8,128)(2,1)S(1)}, u32[]{:S(2)}, u32[]{:S(2)}) collective-permute-start(bf16[2,1040,128]{2,1,0:T(8,128)(2,1)} %add_parts.4.a_ref), channel_id=1, source_target_pairs={{0,2},{1,3},{2,0},{3,1},{4,6},{5,7},{6,4},{7,5},{8,10},{9,11},{10,... | collective-permute-start | bytes 1597448 | tf_op jit(solution)/shard_map/ppermute | solution.py:268
  47.0 0.8 copy-start.1
  49.8 26.3 %collective-permute-start.8 = (bf16[2,1040,128]{2,1,0:T(8,128)(2,1)}, bf16[2,1040,128]{2,1,0:T(8,128)(2,1)S(1)}, u32[]{:S(2)}, u32[]{:S(2)}) collective-permute-start(bf16[2,1040,128]{2,1,0:T(8,128)(2,1)} %add_parts.6.a_ref), channel_id=1, source_target_pairs={{0,2},{1,3},{2,0},{3,1},{4,6},{5,7},{6,4},{7,5},{8,10},{9,11},{10,... | collective-permute-start | bytes 1597448 | tf_op jit(solution)/shard_map/ppermute | solution.py:268
  49.8 0.8 copy-start.2
  52.6 45.9 %collective-permute-start.4 = (bf16[2,1040,128]{2,1,0:T(8,128)(2,1)}, bf16[2,1040,128]{2,1,0:T(8,128)(2,1)}, u32[]{:S(2)}, u32[]{:S(2)}) collective-permute-start(bf16[2,1040,128]{2,1,0:T(8,128)(2,1)} %add_parts.5.total_ref), channel_id=1, source_target_pairs={{0,1},{1,0},{2,3},{3,2},{4,5},{5,4},{6,7},{7,6},{8,9},{9,8},{10,11... | collective-permute-start | bytes 1597448 | tf_op jit(solution)/shard_map/ppermute | solution.py:269
  76.1 17.8 %collective-permute-start.2 = (bf16[1,256,512]{2,1,0:T(8,128)(2,1)S(1)}, bf16[1,256,512]{2,1,0:T(8,128)(2,1)S(1)}, u32[]{:S(2)}, u32[]{:S(2)}) collective-permute-start(bf16[1,256,512]{2,1,0:T(8,128)(2,1)S(1)} %get-tuple-element.12), channel_id=1, source_target_pairs={{0,28},{1,21},{2,30},{3,23},{4,24},{5,17},{6,26},{7,19},{8,20},{9,... | collective-permute-start | bytes 786440 | tf_op jit(solution)/shard_map/ppermute | solution.py:284
  76.1 0.8 copy-start.4
  78.8 10.4 %copy-start.3 = (bf16[2,1040,128]{2,1,0:T(8,128)(2,1)S(1)}, bf16[2,1040,128]{2,1,0:T(8,128)(2,1)}, u32[]{:S(2)}) copy-start(bf16[2,1040,128]{2,1,0:T(8,128)(2,1)} %add_parts.7.total_ref) | copy-start | bytes 1597444
  89.2 25.3 %collective-permute-start.11 = (bf16[2,1040,128]{2,1,0:T(8,128)(2,1)S(1)}, bf16[2,1040,128]{2,1,0:T(8,128)(2,1)}, u32[]{:S(2)}, u32[]{:S(2)}) collective-permute-start(bf16[2,1040,128]{2,1,0:T(8,128)(2,1)S(1)} %copy-done.3), channel_id=1, source_target_pairs={{0,1},{1,0},{2,3},{3,2},{4,5},{5,4},{6,7},{7,6},{8,9},{9,8},{10,11... | collective-permute-start | bytes 1597448 | tf_op jit(solution)/shard_map/ppermute | solution.py:269
  89.2 9.2 %collective-permute-start.3 = (bf16[1,256,512]{2,1,0:T(8,128)(2,1)}, bf16[1,256,512]{2,1,0:T(8,128)(2,1)S(1)}, u32[]{:S(2)}, u32[]{:S(2)}) collective-permute-start(bf16[1,256,512]{2,1,0:T(8,128)(2,1)} %get-tuple-element.11), channel_id=1, source_target_pairs={{0,24},{1,17},{2,26},{3,19},{4,28},{5,21},{6,30},{7,23},{8,16},{9,... | collective-permute-start | bytes 786440 | tf_op jit(solution)/shard_map/ppermute | solution.py:284
  93.3 36.1 %collective-permute-start.9 = (bf16[1,256,512]{2,1,0:T(8,128)(2,1)}, bf16[1,256,512]{2,1,0:T(8,128)(2,1)S(1)}, u32[]{:S(2)}, u32[]{:S(2)}) collective-permute-start(bf16[1,256,512]{2,1,0:T(8,128)(2,1)} %get-tuple-element.8), channel_id=1, source_target_pairs={{0,8},{1,13},{2,10},{3,15},{4,12},{5,9},{6,14},{7,11},{8,0},{9,5},... | collective-permute-start | bytes 786440 | tf_op jit(solution)/shard_map/ppermute | solution.py:284
  93.8 35.6 %collective-permute-start.10 = (bf16[1,256,512]{2,1,0:T(8,128)(2,1)}, bf16[1,256,512]{2,1,0:T(8,128)(2,1)S(1)}, u32[]{:S(2)}, u32[]{:S(2)}) collective-permute-start(bf16[1,256,512]{2,1,0:T(8,128)(2,1)} %get-tuple-element.7), channel_id=1, source_target_pairs={{0,0},{1,5},{2,2},{3,7},{4,4},{5,1},{6,6},{7,3},{8,8},{9,13},{10,1... | collective-permute-start | bytes 786440 | tf_op jit(solution)/shard_map/ppermute | solution.py:284
  110.6 15.3 %collective-permute-start.5 = (bf16[1,256,512]{2,1,0:T(8,128)(2,1)}, bf16[1,256,512]{2,1,0:T(8,128)(2,1)}, u32[]{:S(2)}, u32[]{:S(2)}) collective-permute-start(bf16[1,256,512]{2,1,0:T(8,128)(2,1)} %get-tuple-element.10), channel_id=1, source_target_pairs={{0,20},{1,29},{2,22},{3,31},{4,16},{5,25},{6,18},{7,27},{8,28},{9,... | collective-permute-start | bytes 786440 | tf_op jit(solution)/shard_map/ppermute | solution.py:284
  112.9 16.5 %collective-permute-start.6 = (bf16[1,256,512]{2,1,0:T(8,128)(2,1)}, bf16[1,256,512]{2,1,0:T(8,128)(2,1)S(1)}, u32[]{:S(2)}, u32[]{:S(2)}) collective-permute-start(bf16[1,256,512]{2,1,0:T(8,128)(2,1)} %get-tuple-element.9), channel_id=1, source_target_pairs={{0,16},{1,25},{2,18},{3,27},{4,20},{5,29},{6,22},{7,31},{8,24},{9,... | collective-permute-start | bytes 786440 | tf_op jit(solution)/shard_map/ppermute | solution.py:284
  125.8 7.7 %collective-permute-start.12 = (bf16[1,256,512]{2,1,0:T(8,128)(2,1)S(1)}, bf16[1,256,512]{2,1,0:T(8,128)(2,1)S(1)}, u32[]{:S(2)}, u32[]{:S(2)}) collective-permute-start(bf16[1,256,512]{2,1,0:T(8,128)(2,1)S(1)} %get-tuple-element.6), channel_id=1, source_target_pairs={{0,12},{1,9},{2,14},{3,11},{4,8},{5,13},{6,10},{7,15},{8,4},{9,1},... | collective-permute-start | bytes 786440 | tf_op jit(solution)/shard_map/ppermute | solution.py:284
  125.9 7.7 %collective-permute-start.13 = (bf16[1,256,512]{2,1,0:T(8,128)(2,1)S(1)}, bf16[1,256,512]{2,1,0:T(8,128)(2,1)S(1)}, u32[]{:S(2)}, u32[]{:S(2)}) collective-permute-start(bf16[1,256,512]{2,1,0:T(8,128)(2,1)S(1)} %get-tuple-element.5), channel_id=1, source_target_pairs={{0,4},{1,1},{2,6},{3,3},{4,0},{5,5},{6,2},{7,7},{8,12},{9,9},{10,1... | collective-permute-start | bytes 786440 | tf_op jit(solution)/shard_map/ppermute | solution.py:284
  133.5 1.3 copy-start

commit v2 on v0

v2 whole, which is shorter than its diff:
```python
import functools

import jax
import jax.numpy as jnp
from jax import lax
from jax.experimental import pallas as pl
from jax.experimental.pallas import tpu as pltpu
from jax.sharding import PartitionSpec as P


NS_IT = 4
LANES = 128
EXTRA = 16
F32 = jnp.float32
BF16 = jnp.bfloat16


def block_pairs(blocks):
    return [(i, j) for i in range(blocks) for j in range(i + 1, blocks)]


def packed_rows(members):
    blocks = members // LANES
    return (len(block_pairs(blocks)) + blocks // 2) * LANES + EXTRA


def square_iota():
    row = lax.broadcasted_iota(jnp.int32, (LANES, LANES), 0)
    col = lax.broadcasted_iota(jnp.int32, (LANES, LANES), 1)
    return row, col


def store_packed(out_ref, place, blocks, part, tail):
    row, col = square_iota()
    at = 0
    for i, j in block_pairs(blocks):
        out_ref[place, at:at + LANES] = part(i, j).astype(BF16)
        at += LANES
    sub = lax.broadcasted_iota(jnp.int32, (8, LANES), 0)
    low = tail[8:]
    for i in range(0, blocks, 2):
        second = part(i + 1, i + 1)
        out_ref[place, at:at + LANES] = jnp.where(row <= col, part(i, i), second).astype(BF16)
        at += LANES
        line = jnp.sum(jnp.where(row == col, second, 0.0), axis=0, keepdims=True)
        low = jnp.where(sub == i // 2, line, low)
    out_ref[place, at:at + EXTRA] = jnp.concatenate([tail[:8], low], axis=0).astype(BF16)


def load_packed(buf, k, members):
    blocks = members // LANES
    row, col = square_iota()
    base = packed_rows(members) - EXTRA
    tail = buf[k, base:base + EXTRA].astype(F32)
    grid = {}
    at = 0
    for i, j in block_pairs(blocks):
        part = buf[k, at:at + LANES].astype(F32)
        grid[i, j] = part
        grid[j, i] = jnp.transpose(part)
        at += LANES
    for i in range(0, blocks, 2):
        part = buf[k, at:at + LANES].astype(F32)
        flip = jnp.transpose(part)
        at += LANES
        grid[i, i] = jnp.where(row <= col, part, flip)
        low = jnp.where(row > col, part, flip)
        grid[i + 1, i + 1] = jnp.where(row == col, tail[8 + i // 2:9 + i // 2], low)
    whole = jnp.concatenate(
        [jnp.concatenate([grid[i, j] for j in range(blocks)], axis=1) for i in range(blocks)], axis=0)
    return whole, tail


def split_rows(line, blocks):
    sub = lax.broadcasted_iota(jnp.int32, (8, LANES), 0)
    wide = jnp.zeros((8, LANES), F32)
    for i in range(blocks):
        wide = jnp.where(sub % 4 == i, line[:, i * LANES:(i + 1) * LANES], wide)
    high = wide.astype(BF16).astype(F32)
    return jnp.where(sub < 4, high, wide - high)


def pick_group(dest_ref, plan, slot):
    even_seq, odd_seq, groups, direct = plan
    own_index, grp_index = lax.axis_index("own"), lax.axis_index("grp")
    step = jnp.where(own_index % 2 == 1, odd_seq[slot], even_seq[slot])
    if not direct:
        return step
    target = grp_index ^ step
    found = jnp.int32(0)
    for k in range(groups):
        found = found + jnp.where(dest_ref[grp_index * groups + k] == target, k, 0)
    return found


def gram_kernel(plan, wanted, dest_ref, count_ref, obs_ref, weight_ref, innov_ref, *refs):
    out_refs, (obs_buf, sem) = refs[:len(wanted)], refs[len(wanted):]
    number, slots, members = obs_buf.shape
    blocks = members // LANES
    picked = [pick_group(dest_ref, plan, slot) for slots_here in wanted for slot in slots_here]
    places = [(ref, k) for ref, slots_here in zip(out_refs, wanted) for k in range(len(slots_here))]
    copies = [pltpu.make_async_copy(obs_ref.at[g], obs_buf.at[k], sem.at[k]) for k, g in enumerate(picked)]
    for copy in copies:
        copy.start()

    def own_row(ref, group):
        rows = lax.broadcasted_iota(jnp.int32, ref.shape, 0)
        return jnp.sum(jnp.where(rows == group, ref[...].astype(F32), 0.0), axis=0, keepdims=True)

    columns, sources = [], []
    for group in picked:
        live = lax.broadcasted_iota(jnp.int32, (1, slots), 1) < count_ref[group]
        weight = jnp.where(live, own_row(weight_ref, group), 0.0)
        sources.append((weight * own_row(innov_ref, group)).astype(BF16))
        column = jnp.transpose(jnp.broadcast_to(weight, (LANES, slots)))
        columns.append(jnp.concatenate([column] * blocks, axis=1))
    perts, scaled = [], []
    for k in range(number):
        copies[k].wait()
        obs = obs_buf[k].astype(F32)
        mean = jnp.mean(obs, axis=1, keepdims=True)
        pert = (obs - mean).astype(BF16)
        perts.append(pert)
        scaled.append((pert.astype(F32) * columns[k]).astype(BF16))
    for k in range(number):
        pert, weighted = perts[k], scaled[k]
        out_ref, place = places[k]
        parts = {}
        for i in range(0, blocks, 2):
            strip = lax.dot_general(
                weighted[:, i * LANES:(i + 2) * LANES], pert[:, i * LANES:],
                (((0,), (0,)), ((), ())), preferred_element_type=F32)
            for a in range(2):
                for j in range(i + a, blocks):
                    parts[i + a, j] = strip[a * LANES:(a + 1) * LANES, (j - i) * LANES:(j - i + 1) * LANES]
        rhs = jnp.dot(jnp.broadcast_to(sources[k], (16, slots)), pert, preferred_element_type=F32)[:8]
        tail = jnp.concatenate([split_rows(rhs, blocks), jnp.zeros((8, LANES), F32)], axis=0)
        store_packed(out_ref, place, blocks, lambda i, j: parts[i, j], tail)


def gram_call(obs_ens, weight, innov, dest, count, plan, wanted):
    _, slots, members = obs_ens.shape
    rows = packed_rows(members)
    number = sum(len(slots_here) for slots_here in wanted)
    return pl.pallas_call(
        functools.partial(gram_kernel, plan, wanted),
        out_shape=[jax.ShapeDtypeStruct((len(slots_here), rows, LANES), BF16) for slots_here in wanted],
        in_specs=[
            pl.BlockSpec(memory_space=pltpu.SMEM),
            pl.BlockSpec(memory_space=pltpu.SMEM),
            pl.BlockSpec(memory_space=pl.ANY),
            pl.BlockSpec(memory_space=pltpu.VMEM),
            pl.BlockSpec(memory_space=pltpu.VMEM),
        ],
        out_specs=[pl.BlockSpec(memory_space=pltpu.VMEM)] * len(wanted),
        scratch_shapes=[pltpu.VMEM((number, slots, members), BF16), pltpu.SemaphoreType.DMA((number,))],
        cost_estimate=pl.CostEstimate(
            flops=2 * number * slots * members * members, transcendentals=0,
            bytes_accessed=number * 2 * (slots * members + rows * LANES)),
        name="gram",
    )(dest, count, obs_ens, weight, innov)


def add_parts(a, b):
    rows = a.shape[1]
    main = (a.astype(F32) + b.astype(F32)).astype(BF16)
    tail = a[:, rows - EXTRA:rows - 8].astype(F32) + b[:, rows - EXTRA:rows - 8].astype(F32)
    wide = tail[:, :4] + tail[:, 4:]
    high = lax.reduce_precision(wide, 8, 7)
    split = jnp.concatenate([high, wide - high], axis=1).astype(BF16)
    return lax.dynamic_update_slice(main, split, (0, rows - EXTRA, 0))


def apply_rows(state, weights):
    state = state.astype(F32)
    state_mean = jnp.mean(state, axis=1, keepdims=True)
    state_pert = (state - state_mean).astype(BF16)
    return (state_mean + jnp.dot(state_pert, weights, preferred_element_type=F32)).astype(BF16)


def solve_kernel(plan, offset, number, dest_ref, total_ref, state_ref, *refs):
    out_refs, (total_buf, state_buf, sem, state_sem) = refs[:-4], refs[-4:]
    members = state_buf.shape[2]
    blocks = members // LANES
    fetch = [pltpu.make_async_copy(total_ref.at[k], total_buf.at[k], sem.at[k]) for k in range(number)]
    picked = [pick_group(dest_ref, plan, offset + k) for k in range(number)]
    states = [
        pltpu.make_async_copy(state_ref.at[g], state_buf.at[k], state_sem.at[k]) for k, g in enumerate(picked)]
    for copy in fetch + states:
        copy.start()
    big_row = lax.broadcasted_iota(jnp.int32, (members, members), 0)
    big_col = lax.broadcasted_iota(jnp.int32, (members, members), 1)
    eye = big_row == big_col
    sub = lax.broadcasted_iota(jnp.int32, (16, LANES), 0)

    def mul(a, b):
        return jnp.dot(a, b, preferred_element_type=F32)

    roots, scales, rhs = [], [], []
    for k in range(number):
        fetch[k].wait()
        gram, tail = load_packed(total_buf, k, members)
        matrix = gram + jnp.where(eye, members - 1.0, 0.0)
        square = jnp.sum(matrix * matrix, axis=0, keepdims=True)
        scale = jnp.sqrt(jnp.sum(square, axis=1, keepdims=True))
        scales.append(scale)
        roots.append((matrix / scale).astype(BF16))
        lines = [
            jnp.where(sub == 0, tail[i:i + 1], jnp.where(sub == 1, tail[4 + i:5 + i], 0.0))
            for i in range(blocks)]
        rhs.append(jnp.concatenate(lines, axis=1).astype(BF16))

    inverses = [None] * number
    for iteration in range(NS_IT):
        products = [
            root.astype(F32) if inverse is None else mul(inverse, root) for inverse, root in zip(inverses, roots)]
        factors = [(jnp.where(eye, 1.5, 0.0) - 0.5 * product).astype(BF16) for product in products]
        inverses = [
            factor if inverse is None else mul(factor, inverse).astype(BF16)
            for inverse, factor in zip(inverses, factors)]
        if iteration + 1 < NS_IT:
            roots = [mul(root, factor).astype(BF16) for root, factor in zip(roots, factors)]

    for k in range(number):
        half_way = jnp.sum(mul(rhs[k], inverses[k]), axis=0, keepdims=True)
        wide = inverses[k].astype(F32)
        mean_weight = jnp.sum(wide * half_way, axis=1, keepdims=True) / scales[k]
        spread = jnp.sqrt((members - 1.0) / scales[k])
        if len(out_refs) > number:
            flat = jnp.transpose(jnp.broadcast_to(mean_weight, (members, LANES)))[:1]
            tail = jnp.zeros((8, LANES), F32)
            left = jnp.broadcast_to(spread, (8, LANES))
            for place in range(4, 7):
                term = left.astype(BF16).astype(F32)
                tail = jnp.where(sub[:8] == place, term, tail)
                left = left - term
            tail = jnp.concatenate([split_rows(flat, blocks), tail], axis=0)
            store_packed(
                out_refs[number], k, blocks,
                lambda i, j: wide[i * LANES:(i + 1) * LANES, j * LANES:(j + 1) * LANES], tail)
        weights = (spread * wide + mean_weight).astype(BF16)
        states[k].wait()
        out_refs[k][0] = apply_rows(state_buf[k], weights)


def apply_kernel(plan, offset, number, dest_ref, packed_ref, state_ref, *refs):
    out_refs, (packed_buf, state_buf, sem, state_sem) = refs[:-4], refs[-4:]
    members = state_buf.shape[2]
    blocks = members // LANES
    fetch = [pltpu.make_async_copy(packed_ref.at[k], packed_buf.at[k], sem.at[k]) for k in range(number)]
    picked = [pick_group(dest_ref, plan, offset + k) for k in range(number)]
    states = [
        pltpu.make_async_copy(state_ref.at[g], state_buf.at[k], state_sem.at[k]) for k, g in enumerate(picked)]
    for copy in fetch + states:
        copy.start()
    for k in range(number):
        fetch[k].wait()
        inverse, tail = load_packed(packed_buf, k, members)
        spread = tail[12:13, :1] + tail[13:14, :1] + tail[14:15, :1]
        means = tail[:8] + pltpu.roll(tail[:8], 4, 0)
        column = jnp.concatenate(
            [jnp.transpose(jnp.broadcast_to(means[i:i + 1], (LANES, LANES))) for i in range(blocks)], axis=0)
        column = jnp.concatenate([column] * blocks, axis=1)
        weights = (spread * inverse + column).astype(BF16)
        states[k].wait()
        out_refs[k][0] = apply_rows(state_buf[k], weights)


def solve_call(total, background, dest, plan, offset, kernel, emit):
    number, rows, lanes = total.shape
    here, members = background.shape[1:]
    products = 3 * NS_IT - 3 if kernel is solve_kernel else 1
    packed = [jax.ShapeDtypeStruct((number, rows, lanes), BF16)] if emit else []
    return pl.pallas_call(
        functools.partial(kernel, plan, offset, number),
        out_shape=[jax.ShapeDtypeStruct((1, here, members), BF16)] * number + packed,
        in_specs=[
            pl.BlockSpec(memory_space=pltpu.SMEM),
            pl.BlockSpec(memory_space=pl.ANY),
            pl.BlockSpec(memory_space=pl.ANY),
        ],
        out_specs=[pl.BlockSpec(memory_space=pltpu.VMEM)] * (number + len(packed)),
        scratch_shapes=[
            pltpu.VMEM((number, rows, lanes), BF16), pltpu.VMEM((number, here, members), BF16),
            pltpu.SemaphoreType.DMA((number,)), pltpu.SemaphoreType.DMA((number,))],
        cost_estimate=pl.CostEstimate(
            flops=number * products * 2 * members ** 3, transcendentals=0,
            bytes_accessed=number * (2 * rows * lanes + 4 * here * members)),
        name="solve" if kernel is solve_kernel else "apply",
    )(dest, total, background)


def pack_rows(array_in, send_index, send_live):
    picked = jnp.take(array_in, send_index, axis=0)
    keep_mask = send_live.reshape((-1,) + (1,) * (array_in.ndim - 1))
    return jnp.where(keep_mask, picked, jnp.zeros_like(picked))


def send_all(result, dest, my_dest, grp_size, grp_index):
    local_groups = result.shape[0]
    group_ids = jnp.arange(dest.shape[0], dtype=jnp.int32)
    same_dest = dest[None, :] == dest[:, None]
    earlier = group_ids[None, :] < group_ids[:, None]
    arrival_rank = jnp.sum(jnp.where(same_dest & earlier, 1, 0), axis=1).astype(jnp.int32)
    peer_ids = jnp.arange(grp_size, dtype=jnp.int32)
    local_ids = jnp.arange(local_groups, dtype=jnp.int32)
    peer_hits = my_dest[None, :] == peer_ids[:, None]
    send_index = jnp.sum(jnp.where(peer_hits, local_ids[None, :], 0), axis=1)
    send_live = jnp.any(peer_hits, axis=1)
    arriving = (dest[None, :] == grp_index) & (arrival_rank[None, :] == local_ids[:, None])
    arrive_group = jnp.sum(jnp.where(arriving, group_ids[None, :], 0), axis=1)
    received = lax.all_to_all(
        pack_rows(result, send_index, send_live), "grp", split_axis=0, concat_axis=0, tiled=True)
    return jnp.take(received, arrive_group // local_groups, axis=0)


def body(background, obs_ens, innovation, obs_weight, obs_count, dest):
    grp_size, own_size = lax.axis_size("grp"), lax.axis_size("own")
    grp_index, own_index = lax.axis_index("grp"), lax.axis_index("own")
    groups = background.shape[0]
    odd = own_index % 2
    quarter = groups // 8
    sizes = [quarter, groups // 2 - 2 * quarter, quarter]
    even_seq, odd_seq, slots, at = [], [], [], 0
    far = list(range(groups - 1, -1, -1))
    for size in sizes:
        block = far[2 * at:2 * (at + size)]
        even_seq += block[0::2] + block[1::2]
        odd_seq += block[1::2] + block[0::2]
        slots.append((tuple(range(2 * at, 2 * at + size)), tuple(range(2 * at + size, 2 * (at + size)))))
        at += size
    direct = grp_size == groups and groups & (groups - 1) == 0
    plan = (tuple(even_seq), tuple(odd_seq), groups, direct)

    count = obs_count.reshape(groups)
    pair = [(i, i ^ 1) for i in range(own_size)]
    crosses = []
    while 2 << len(crosses) < own_size:
        step = 2 << len(crosses)
        crosses.append([(i, i ^ step) for i in range(own_size)])

    def gram(wanted):
        return gram_call(obs_ens, obs_weight, innovation, dest, count, plan, wanted)

    sends, keeps = [None] * 3, [None] * 3
    sends[0], = gram((slots[0][1],))
    keeps[0], sends[1] = gram((slots[0][0], slots[1][1]))
    keeps[1], sends[2], keeps[2] = gram((slots[1][0], slots[2][1], slots[2][0]))
    results = [None] * groups
    for chunk, (kept, given) in enumerate(slots):
        arrived = lax.ppermute(sends[chunk], "own", pair)
        mine = add_parts(keeps[chunk], arrived)
        for cross in crosses:
            arrived = lax.ppermute(mine, "own", cross)
            mine = add_parts(mine, arrived)
        last = chunk == 2
        if last:
            other = lax.ppermute(mine, "own", pair)
        solved = solve_call(mine, background, dest, plan, kept[0], solve_kernel, not last)
        if not last:
            other = lax.ppermute(solved[-1], "own", pair)
        results[kept[0]:kept[0] + len(kept)] = solved[:len(kept)]
        results[given[0]:given[0] + len(given)] = solve_call(
            other, background, dest, plan, given[0], solve_kernel if last else apply_kernel, False)
    if not direct:
        even_back, odd_back = ([seq.index(k) for k in range(groups)] for seq in (even_seq, odd_seq))
        back = jnp.where(odd == 1, jnp.array(odd_back, jnp.int32), jnp.array(even_back, jnp.int32))
        result = jnp.take(jnp.concatenate(results, axis=0), back, axis=0)
        my_dest = lax.dynamic_slice_in_dim(dest, grp_index * groups, groups)
        return send_all(result, dest, my_dest, grp_size, grp_index)
    out = jnp.zeros(background.shape, background.dtype)
    arrivals, sources = [], []
    for slot, done in enumerate(results):
        pairs = []
        for i in range(grp_size):
            for o in range(own_size):
                step = (odd_seq if o % 2 else even_seq)[slot]
                pairs.append((i * own_size + o, (i ^ step) * own_size + o))
        arrivals.append(lax.ppermute(done, ("grp", "own"), pairs))
        sources.append(grp_index ^ jnp.where(odd == 1, odd_seq[slot], even_seq[slot]))
    late, _ = lax.optimization_barrier((tuple(arrivals[:-1]), results[-1]))
    for arrived, source in zip(late + (arrivals[-1],), sources):
        out = lax.dynamic_update_slice_in_dim(out, arrived, source, 0)
    return out


def solution(mesh):
    return mapped(mesh)


def mapped(mesh):
    return jax.shard_map(
        body,
        mesh=mesh,
        in_specs=(
            P("grp", "own", None),
            P("grp", "own", None),
            P("grp", "own"),
            P("grp", "own"),
            P("grp", "own"),
            P(),
        ),
        out_specs=P("grp", "own", None),
        check_vma=False,
    )
```

time: 317 us -> 132 us (0.42)
  waiting for transfers between devices: 228 us -> 52 us
  Pallas kernels: 0 us -> 47.1 us
  matrix products: 28.4 us -> 0 us
  starting transfers between devices: 3.7 us -> 26.2 us
  blocking collectives: 21.8 us -> 0 us
  between operations: 14.3 us -> 0.57 us
  other arithmetic: 13.2 us -> 0.8 us
    reduce_scatter x1 -> x0, waiting for transfers between devices: 121 us -> none  [solve_weights(): lax.psum_scatter(gram_local, 'own', scatter_dimension=0, tiled=True)]
    all_gather x1 -> x0, waiting for transfers between devices: 80.8 us -> none  [solve_weights(): lax.all_gather(newton_weights(gram_part, right_part), 'own', axis=0, tile...]
    ppermute x0 -> x17, waiting for transfers between devices: none -> 52 us  [the longest x3 31.5 us: body(): arrived = lax.ppermute(mine, 'own', cross)]
    pallas_call x0 -> x9, Pallas kernels: none -> 47.1 us  [the longest x6 35.2 us: solve_call(): pl.pallas_call(functools.partial(kernel, plan, offset, number), out_shape...]
    dot_general x15 -> x0, matrix products: 28.4 us -> none  [the longest x1 6.28 us: solve_weights(): jnp.einsum('gpk,gpl->gkl', weighted, obs_pert, preferred_element_type=jnp...]
    all_to_all x1 -> x0, waiting for transfers between devices: 26.3 us -> none  [body(): lax.all_to_all(pack_rows(result, send_index, send_live), 'grp', split_axi...]
    ppermute x0 -> x17, starting transfers between devices: none -> 26.2 us  [the longest x8 11.7 us: body(): arrivals.append(lax.ppermute(done, ('grp', 'own'), pairs))]
    unnamed x1 -> x0, blocking collectives: 21.8 us -> none
  transfers between devices with their start and end apart: 3 -> 17, of which waited for: 3 -> 4; matrix products, arithmetic and copies ran while one was open for 1% -> 1% of each run, Pallas kernels for 0% -> 32%
where the time goes in v2:
time: 132 us; the launch traced here: 131 us
  waiting for transfers between devices  52 us (39%)
  Pallas kernels  47.1 us (36%)
  starting transfers between devices  26.2 us (20%)
  local copies, waits for them, and re-layouts  4.62 us (4%)
    pallas_call x6, Pallas kernels, solve_call(): pl.pallas_call(functools.partial(kernel, plan, offset, number), out_shape...  35.2 us
    ppermute x3, waiting for transfers between devices, body(): arrived = lax.ppermute(mine, 'own', cross)  31.5 us
    ppermute x3, waiting for transfers between devices, body(): arrived = lax.ppermute(sends[chunk], 'own', pair)  17.2 us
    pallas_call x3, Pallas kernels, gram_call(): pl.pallas_call(functools.partial(gram_kernel, plan, wanted), out_shape=[j...  11.9 us
    ppermute x8, starting transfers between devices, body(): arrivals.append(lax.ppermute(done, ('grp', 'own'), pairs))  11.7 us
    ppermute x3, starting transfers between devices, body(): arrived = lax.ppermute(sends[chunk], 'own', pair)  5.2 us
    ppermute x3, starting transfers between devices, body(): arrived = lax.ppermute(mine, 'own', cross)  4.76 us
    unnamed x26, local copies, waits for them, and re-layouts  3.55 us
  transfers between devices with their start and end apart: 17, of which 4 were waited for; matrix products, arithmetic and copies ran while one was open for 1% of the time, Pallas kernels for 32%

profile of v2, /device:TPU:0, one launch (start us, length us, event | category | flops | bytes accessed | tf_op | source)
XLA Modules:
  0.0 131.3 jit_solution(14154490245925811059)
XLA Ops:
  0.0 4.6 %gram.5 = (bf16[2,1040,128]{2,1,0:T(8,128)(2,1)}, bf16[1,1040,128]{2,1,0:T(8,128)(2,1)}, bf16[1,1040,128]{2,1,0:T(8,128)(2,1)}) custom-call(s32[64]{0:T(128)} %dest_ref.17, s32[8]{0:T(128)} %bitcast.1, bf16[8,512,512]{2,1,0:T(8,128)(2,1)} %obs_ref.5, bf16[8,512]{1,0:T(8,128)(2,1)} %weight_ref.5, bf16[8,512]{1,0:T(8,128)(2,1)} %innov_ref.5), custom_call_target="tpu_custom_call" | custom-call | flops 1073741824 | bytes 3162112 | tf_op jit(solution)/shard_map/gram/pallas_call | solution.py:145
  4.6 3.1 %collective-permute-start.12 = (bf16[1,1040,128]{2,1,0:T(8,128)(2,1)}, bf16[1,1040,128]{2,1,0:T(8,128)(2,1)S(1)}, u32[]{:S(2)}, u32[]{:S(2)}) collective-permute-start(bf16[1,1040,128]{2,1,0:T(8,128)(2,1)} %get-tuple-element.35), channel_id=1, source_target_pairs={{0,1},{1,0},{2,3},{3,2},{4,5},{5,4},{6,7},{7,6},{8,9},{9,8},{10,11... | collective-permute-start | bytes 798728 | tf_op jit(solution)/shard_map/ppermute | solution.py:351
  7.7 4.1 %gram.3 = (bf16[1,1040,128]{2,1,0:T(8,128)(2,1)}, bf16[2,1040,128]{2,1,0:T(8,128)(2,1)}) custom-call(s32[64]{0:T(128)} %dest_ref.17, s32[8]{0:T(128)} %bitcast.2, bf16[8,512,512]{2,1,0:T(8,128)(2,1)} %obs_ref.5, bf16[8,512]{1,0:T(8,128)(2,1)} %weight_ref.5, bf16[8,512]{1,0:T(8,128)(2,1)} %innov_ref.5), custom_call_target="tpu_custom_call" | custom-call | flops 805306368 | bytes 2371584 | tf_op jit(solution)/shard_map/gram/pallas_call | solution.py:145
  11.9 3.2 %gram.4 = bf16[1,1040,128]{2,1,0:T(8,128)(2,1)} custom-call(s32[64]{0:T(128)} %dest_ref.17, s32[8]{0:T(128)} %bitcast.3, bf16[8,512,512]{2,1,0:T(8,128)(2,1)} %obs_ref.5, bf16[8,512]{1,0:T(8,128)(2,1)} %weight_ref.5, bf16[8,512]{1,0:T(8,128)(2,1)} %innov_ref.5), custom_call_target="tpu_custom_call" | custom-call | flops 268435456 | bytes 790528 | tf_op jit(solution)/shard_map/gram/pallas_call | solution.py:145
  15.2 2.0 %collective-permute-start = (bf16[1,1040,128]{2,1,0:T(8,128)(2,1)}, bf16[1,1040,128]{2,1,0:T(8,128)(2,1)S(1)}, u32[]{:S(2)}, u32[]{:S(2)}) collective-permute-start(bf16[1,1040,128]{2,1,0:T(8,128)(2,1)} %gram.4), channel_id=1, source_target_pairs={{0,1},{1,0},{2,3},{3,2},{4,5},{5,4},{6,7},{7,6},{8,9},{9,8},{10,11... | collective-permute-start | bytes 798728 | tf_op jit(solution)/shard_map/ppermute | solution.py:351
  17.3 2.6 %collective-permute-start.13 = (bf16[1,1040,128]{2,1,0:T(8,128)(2,1)S(1)}, bf16[1,1040,128]{2,1,0:T(8,128)(2,1)S(1)}, u32[]{:S(2)}, u32[]{:S(2)}) collective-permute-start(bf16[1,1040,128]{2,1,0:T(8,128)(2,1)S(1)} %constant_dynamic-update-slice_fusion.9), channel_id=1, source_target_pairs={{0,2},{1,3},{2,0},{3,1},{4,6},{5,7},{6,4},{7,5},{8,10},{9,11},{10,... | collective-permute-start | bytes 798728 | tf_op jit(solution)/shard_map/ppermute | solution.py:354
  19.9 17.2 %collective-permute-done = bf16[1,1040,128]{2,1,0:T(8,128)(2,1)S(1)} collective-permute-done((bf16[1,1040,128]{2,1,0:T(8,128)(2,1)}, bf16[1,1040,128]{2,1,0:T(8,128)(2,1)S(1)}, u32[]{:S(2)}, u32[]{:S(2)}) %collective-permute-start) | collective-permute-done | bytes 266272 | tf_op jit(solution)/shard_map/ppermute | solution.py:351
  37.2 2.0 %collective-permute-start.1 = (bf16[1,1040,128]{2,1,0:T(8,128)(2,1)S(1)}, bf16[1,1040,128]{2,1,0:T(8,128)(2,1)S(1)}, u32[]{:S(2)}, u32[]{:S(2)}) collective-permute-start(bf16[1,1040,128]{2,1,0:T(8,128)(2,1)S(1)} %constant_dynamic-update-slice_fusion.12), channel_id=1, source_target_pairs={{0,2},{1,3},{2,0},{3,1},{4,6},{5,7},{6,4},{7,5},{8,10},{9,11},{10,... | collective-permute-start | bytes 798728 | tf_op jit(solution)/shard_map/ppermute | solution.py:354
  39.4 2.4 %collective-permute-start.15 = (bf16[1,1040,128]{2,1,0:T(8,128)(2,1)S(1)}, bf16[1,1040,128]{2,1,0:T(8,128)(2,1)S(1)}, u32[]{:S(2)}, u32[]{:S(2)}) collective-permute-start(bf16[1,1040,128]{2,1,0:T(8,128)(2,1)S(1)} %constant_dynamic-update-slice_fusion.8.total_ref), channel_id=1, source_target_pairs={{0,1},{1,0},{2,3},{3,2},{4,5},{5,4},{6,7},{7,6},{8,9},{9,8},{10,11... | collective-permute-start | bytes 798728 | tf_op jit(solution)/shard_map/ppermute | solution.py:358
  42.1 12.0 %collective-permute-done.1 = bf16[1,1040,128]{2,1,0:T(8,128)(2,1)S(1)} collective-permute-done((bf16[1,1040,128]{2,1,0:T(8,128)(2,1)S(1)}, bf16[1,1040,128]{2,1,0:T(8,128)(2,1)S(1)}, u32[]{:S(2)}, u32[]{:S(2)}) %collective-permute-start.1) | collective-permute-done | bytes 266272 | tf_op jit(solution)/shard_map/ppermute | solution.py:354
  54.2 19.5 %collective-permute-done.6 = bf16[2,1040,128]{2,1,0:T(8,128)(2,1)S(1)} collective-permute-done((bf16[2,1040,128]{2,1,0:T(8,128)(2,1)S(1)}, bf16[2,1040,128]{2,1,0:T(8,128)(2,1)S(1)}, u32[]{:S(2)}, u32[]{:S(2)}) %collective-permute-start.6) | collective-permute-done | bytes 532512 | tf_op jit(solution)/shard_map/ppermute | solution.py:354
  74.0 0.8 copy-done.2
  74.8 9.7 %solve.5 = (bf16[1,256,512]{2,1,0:T(8,128)(2,1)}, bf16[1,256,512]{2,1,0:T(8,128)(2,1)}, bf16[2,1040,128]{2,1,0:T(8,128)(2,1)}) custom-call(s32[64]{0:T(128)} %dest_ref.17, bf16[2,1040,128]{2,1,0:T(8,128)(2,1)} %copy-done.2, bf16[8,256,512]{2,1,0:T(8,128)(2,1)} %state_ref.11), custom_call_target="tpu_custom_call" | custom-call | flops 4831838208 | bytes 1581056 | tf_op jit(solution)/shard_map/solve/pallas_call | solution.py:274
  84.7 0.3 collective-permute-start.9
  85.1 6.4 %solve.4 = (bf16[1,256,512]{2,1,0:T(8,128)(2,1)}, bf16[1,1040,128]{2,1,0:T(8,128)(2,1)}) custom-call(s32[64]{0:T(128)} %dest_ref.17, bf16[1,1040,128]{2,1,0:T(8,128)(2,1)} %copy-done.7, bf16[8,256,512]{2,1,0:T(8,128)(2,1)} %state_ref.11), custom_call_target="tpu_custom_call" | custom-call | flops 2415919104 | bytes 790528 | tf_op jit(solution)/shard_map/solve/pallas_call | solution.py:274
  91.5 1.8 %collective-permute-start.3 = (bf16[1,1040,128]{2,1,0:T(8,128)(2,1)}, bf16[1,1040,128]{2,1,0:T(8,128)(2,1)S(1)}, u32[]{:S(2)}, u32[]{:S(2)}) collective-permute-start(bf16[1,1040,128]{2,1,0:T(8,128)(2,1)} %get-tuple-element.26), channel_id=1, source_target_pairs={{0,1},{1,0},{2,3},{3,2},{4,5},{5,4},{6,7},{7,6},{8,9},{9,8},{10,11... | collective-permute-start | bytes 798728 | tf_op jit(solution)/shard_map/ppermute | solution.py:361
  93.3 6.3 %solve.6 = bf16[1,256,512]{2,1,0:T(8,128)(2,1)} custom-call(s32[64]{0:T(128)} %dest_ref.17, bf16[1,1040,128]{2,1,0:T(8,128)(2,1)} %copy-done.6, bf16[8,256,512]{2,1,0:T(8,128)(2,1)} %state_ref.11), custom_call_target="tpu_custom_call" | custom-call | flops 2415919104 | bytes 790528 | tf_op jit(solution)/shard_map/solve/pallas_call | solution.py:274
  99.6 2.1 %collective-permute-start.14 = (bf16[1,256,512]{2,1,0:T(8,128)(2,1)}, bf16[1,256,512]{2,1,0:T(8,128)(2,1)S(1)}, u32[]{:S(2)}, u32[]{:S(2)}) collective-permute-start(bf16[1,256,512]{2,1,0:T(8,128)(2,1)} %solve.6), channel_id=1, source_target_pairs={{0,4},{1,1},{2,6},{3,3},{4,0},{5,5},{6,2},{7,7},{8,12},{9,9},{10,1... | collective-permute-start | bytes 786440 | tf_op jit(solution)/shard_map/ppermute | solution.py:379
  101.7 2.9 %collective-permute-start.2 = (bf16[1,256,512]{2,1,0:T(8,128)(2,1)S(1)}, bf16[1,256,512]{2,1,0:T(8,128)(2,1)S(1)}, u32[]{:S(2)}, u32[]{:S(2)}) collective-permute-start(bf16[1,256,512]{2,1,0:T(8,128)(2,1)S(1)} %copy-done.12), channel_id=1, source_target_pairs={{0,28},{1,25},{2,30},{3,27},{4,24},{5,29},{6,26},{7,31},{8,20},{9,... | collective-permute-start | bytes 786440 | tf_op jit(solution)/shard_map/ppermute | solution.py:379
  104.6 0.7 copy-done.8
  105.3 2.9 %apply.2 = bf16[1,256,512]{2,1,0:T(8,128)(2,1)} custom-call(s32[64]{0:T(128)} %dest_ref.17, bf16[1,1040,128]{2,1,0:T(8,128)(2,1)} %copy-done.8, bf16[8,256,512]{2,1,0:T(8,128)(2,1)} %state_ref.11), custom_call_target="tpu_custom_call" | custom-call | flops 268435456 | bytes 790528 | tf_op jit(solution)/shard_map/apply/pallas_call | solution.py:274
  108.3 1.9 %collective-permute-start.4 = (bf16[1,256,512]{2,1,0:T(8,128)(2,1)}, bf16[1,256,512]{2,1,0:T(8,128)(2,1)S(1)}, u32[]{:S(2)}, u32[]{:S(2)}) collective-permute-start(bf16[1,256,512]{2,1,0:T(8,128)(2,1)} %apply.2), channel_id=1, source_target_pairs={{0,24},{1,29},{2,26},{3,31},{4,28},{5,25},{6,30},{7,27},{8,16},{9,... | collective-permute-start | bytes 786440 | tf_op jit(solution)/shard_map/ppermute | solution.py:379
  110.3 0.7 copy-done.3
  111.0 3.5 %apply.3 = (bf16[1,256,512]{2,1,0:T(8,128)(2,1)}, bf16[1,256,512]{2,1,0:T(8,128)(2,1)}) custom-call(s32[64]{0:T(128)} %dest_ref.17, bf16[2,1040,128]{2,1,0:T(8,128)(2,1)} %copy-done.3, bf16[8,256,512]{2,1,0:T(8,128)(2,1)} %state_ref.11), custom_call_target="tpu_custom_call" | custom-call | flops 536870912 | bytes 1581056 | tf_op jit(solution)/shard_map/apply/pallas_call | solution.py:274
  114.6 0.7 collective-permute-start.8
  115.3 0.9 collective-permute-start.10
  116.2 1.5 %collective-permute-start.11 = (bf16[1,256,512]{2,1,0:T(8,128)(2,1)}, bf16[1,256,512]{2,1,0:T(8,128)(2,1)S(1)}, u32[]{:S(2)}, u32[]{:S(2)}) collective-permute-start(bf16[1,256,512]{2,1,0:T(8,128)(2,1)} %get-tuple-element.33), channel_id=1, source_target_pairs={{0,8},{1,13},{2,10},{3,15},{4,12},{5,9},{6,14},{7,11},{8,0},{9,5},... | collective-permute-start | bytes 786440 | tf_op jit(solution)/shard_map/ppermute | solution.py:379
  117.7 6.3 %solve.7 = bf16[1,256,512]{2,1,0:T(8,128)(2,1)} custom-call(s32[64]{0:T(128)} %dest_ref.17, bf16[1,1040,128]{2,1,0:T(8,128)(2,1)} %copy-done.9, bf16[8,256,512]{2,1,0:T(8,128)(2,1)} %state_ref.11), custom_call_target="tpu_custom_call" | custom-call | flops 2415919104 | bytes 790528 | tf_op jit(solution)/shard_map/solve/pallas_call | solution.py:274
  124.0 1.6 %collective-permute-start.16 = (bf16[1,256,512]{2,1,0:T(8,128)(2,1)}, bf16[1,256,512]{2,1,0:T(8,128)(2,1)S(1)}, u32[]{:S(2)}, u32[]{:S(2)}) collective-permute-start(bf16[1,256,512]{2,1,0:T(8,128)(2,1)} %solve.7), channel_id=1, source_target_pairs={{0,0},{1,5},{2,2},{3,7},{4,4},{5,1},{6,6},{7,3},{8,8},{9,13},{10,1... | collective-permute-start | bytes 786440 | tf_op jit(solution)/shard_map/ppermute | solution.py:379
  125.6 3.2 %collective-permute-done.10 = bf16[1,256,512]{2,1,0:T(8,128)(2,1)S(1)} collective-permute-done((bf16[1,256,512]{2,1,0:T(8,128)(2,1)}, bf16[1,256,512]{2,1,0:T(8,128)(2,1)S(1)}, u32[]{:S(2)}, u32[]{:S(2)}) %collective-permute-start.10) | collective-permute-done | bytes 262176 | tf_op jit(solution)/shard_map/ppermute | solution.py:379
  129.3 1.3 copy-done
  130.6 0.7 constant_dynamic-update-slice_fusion
  (70 shorter events, 1.5 us)
Async XLA Ops:
  4.6 12.6 %collective-permute-start.12 = (bf16[1,1040,128]{2,1,0:T(8,128)(2,1)}, bf16[1,1040,128]{2,1,0:T(8,128)(2,1)S(1)}, u32[]{:S(2)}, u32[]{:S(2)}) collective-permute-start(bf16[1,1040,128]{2,1,0:T(8,128)(2,1)} %get-tuple-element.35), channel_id=1, source_target_pairs={{0,1},{1,0},{2,3},{3,2},{4,5},{5,4},{6,7},{7,6},{8,9},{9,8},{10,11... | collective-permute-start | bytes 798728 | tf_op jit(solution)/shard_map/ppermute | solution.py:351
  11.8 5.3 %copy-start.5 = (bf16[1,1040,128]{2,1,0:T(8,128)(2,1)S(1)}, bf16[1,1040,128]{2,1,0:T(8,128)(2,1)}, u32[]{:S(2)}) copy-start(bf16[1,1040,128]{2,1,0:T(8,128)(2,1)} %get-tuple-element.34) | copy-start | bytes 798724
  11.8 25.3 %copy-start.4 = (bf16[1,1040,128]{2,1,0:T(8,128)(2,1)S(1)}, bf16[1,1040,128]{2,1,0:T(8,128)(2,1)}, u32[]{:S(2)}) copy-start(bf16[1,1040,128]{2,1,0:T(8,128)(2,1)} %get-tuple-element.24) | copy-start | bytes 798724
  11.8 30.0 %collective-permute-start.5 = (bf16[2,1040,128]{2,1,0:T(8,128)(2,1)}, bf16[2,1040,128]{2,1,0:T(8,128)(2,1)S(1)}, u32[]{:S(2)}, u32[]{:S(2)}) collective-permute-start(bf16[2,1040,128]{2,1,0:T(8,128)(2,1)} %get-tuple-element.28), channel_id=1, source_target_pairs={{0,1},{1,0},{2,3},{3,2},{4,5},{5,4},{6,7},{7,6},{8,9},{9,8},{10,11... | collective-permute-start | bytes 1597448 | tf_op jit(solution)/shard_map/ppermute | solution.py:351
  15.2 26.7 %copy-start.1 = (bf16[2,1040,128]{2,1,0:T(8,128)(2,1)S(1)}, bf16[2,1040,128]{2,1,0:T(8,128)(2,1)}, u32[]{:S(2)}) copy-start(bf16[2,1040,128]{2,1,0:T(8,128)(2,1)} %get-tuple-element.27) | copy-start | bytes 1597444
  15.2 21.9 %collective-permute-start = (bf16[1,1040,128]{2,1,0:T(8,128)(2,1)}, bf16[1,1040,128]{2,1,0:T(8,128)(2,1)S(1)}, u32[]{:S(2)}, u32[]{:S(2)}) collective-permute-start(bf16[1,1040,128]{2,1,0:T(8,128)(2,1)} %gram.4), channel_id=1, source_target_pairs={{0,1},{1,0},{2,3},{3,2},{4,5},{5,4},{6,7},{7,6},{8,9},{9,8},{10,11... | collective-permute-start | bytes 798728 | tf_op jit(solution)/shard_map/ppermute | solution.py:351
  17.3 22.0 %collective-permute-start.13 = (bf16[1,1040,128]{2,1,0:T(8,128)(2,1)S(1)}, bf16[1,1040,128]{2,1,0:T(8,128)(2,1)S(1)}, u32[]{:S(2)}, u32[]{:S(2)}) collective-permute-start(bf16[1,1040,128]{2,1,0:T(8,128)(2,1)S(1)} %constant_dynamic-update-slice_fusion.9), channel_id=1, source_target_pairs={{0,2},{1,3},{2,0},{3,1},{4,6},{5,7},{6,4},{7,5},{8,10},{9,11},{10,... | collective-permute-start | bytes 798728 | tf_op jit(solution)/shard_map/ppermute | solution.py:354
  37.2 16.9 %collective-permute-start.1 = (bf16[1,1040,128]{2,1,0:T(8,128)(2,1)S(1)}, bf16[1,1040,128]{2,1,0:T(8,128)(2,1)S(1)}, u32[]{:S(2)}, u32[]{:S(2)}) collective-permute-start(bf16[1,1040,128]{2,1,0:T(8,128)(2,1)S(1)} %constant_dynamic-update-slice_fusion.12), channel_id=1, source_target_pairs={{0,2},{1,3},{2,0},{3,1},{4,6},{5,7},{6,4},{7,5},{8,10},{9,11},{10,... | collective-permute-start | bytes 798728 | tf_op jit(solution)/shard_map/ppermute | solution.py:354
  39.4 45.2 %copy-start.6 = (bf16[1,1040,128]{2,1,0:T(8,128)(2,1)}, bf16[1,1040,128]{2,1,0:T(8,128)(2,1)S(1)}, u32[]{:S(2)}) copy-start(bf16[1,1040,128]{2,1,0:T(8,128)(2,1)S(1)} %constant_dynamic-update-slice_fusion.8.total_ref) | copy-start | bytes 798724
  39.4 76.8 %collective-permute-start.15 = (bf16[1,1040,128]{2,1,0:T(8,128)(2,1)S(1)}, bf16[1,1040,128]{2,1,0:T(8,128)(2,1)S(1)}, u32[]{:S(2)}, u32[]{:S(2)}) collective-permute-start(bf16[1,1040,128]{2,1,0:T(8,128)(2,1)S(1)} %constant_dynamic-update-slice_fusion.8.total_ref), channel_id=1, source_target_pairs={{0,1},{1,0},{2,3},{3,2},{4,5},{5,4},{6,7},{7,6},{8,9},{9,8},{10,11... | collective-permute-start | bytes 798728 | tf_op jit(solution)/shard_map/ppermute | solution.py:358
  42.0 31.8 %collective-permute-start.6 = (bf16[2,1040,128]{2,1,0:T(8,128)(2,1)S(1)}, bf16[2,1040,128]{2,1,0:T(8,128)(2,1)S(1)}, u32[]{:S(2)}, u32[]{:S(2)}) collective-permute-start(bf16[2,1040,128]{2,1,0:T(8,128)(2,1)S(1)} %constant_dynamic-update-slice_fusion.10), channel_id=1, source_target_pairs={{0,2},{1,3},{2,0},{3,1},{4,6},{5,7},{6,4},{7,5},{8,10},{9,11},{10,... | collective-permute-start | bytes 1597448 | tf_op jit(solution)/shard_map/ppermute | solution.py:354
  54.2 30.5 %copy-start.7 = (bf16[1,1040,128]{2,1,0:T(8,128)(2,1)}, bf16[1,1040,128]{2,1,0:T(8,128)(2,1)S(1)}, u32[]{:S(2)}) copy-start(bf16[1,1040,128]{2,1,0:T(8,128)(2,1)S(1)} %constant_dynamic-update-slice_fusion.11.total_ref) | copy-start | bytes 798724
  74.0 0.8 copy-start.2
  84.7 25.5 %collective-permute-start.9 = (bf16[2,1040,128]{2,1,0:T(8,128)(2,1)}, bf16[2,1040,128]{2,1,0:T(8,128)(2,1)S(1)}, u32[]{:S(2)}, u32[]{:S(2)}) collective-permute-start(bf16[2,1040,128]{2,1,0:T(8,128)(2,1)} %get-tuple-element.31), channel_id=1, source_target_pairs={{0,1},{1,0},{2,3},{3,2},{4,5},{5,4},{6,7},{7,6},{8,9},{9,8},{10,11... | collective-permute-start | bytes 1597448 | tf_op jit(solution)/shard_map/ppermute | solution.py:361
  91.4 10.2 %copy-start.12 = (bf16[1,256,512]{2,1,0:T(8,128)(2,1)S(1)}, bf16[1,256,512]{2,1,0:T(8,128)(2,1)}, u32[]{:S(2)}) copy-start(bf16[1,256,512]{2,1,0:T(8,128)(2,1)} %get-tuple-element.25) | copy-start | bytes 786436
  91.5 13.2 %collective-permute-start.3 = (bf16[1,1040,128]{2,1,0:T(8,128)(2,1)}, bf16[1,1040,128]{2,1,0:T(8,128)(2,1)S(1)}, u32[]{:S(2)}, u32[]{:S(2)}) collective-permute-start(bf16[1,1040,128]{2,1,0:T(8,128)(2,1)} %get-tuple-element.26), channel_id=1, source_target_pairs={{0,1},{1,0},{2,3},{3,2},{4,5},{5,4},{6,7},{7,6},{8,9},{9,8},{10,11... | collective-permute-start | bytes 798728 | tf_op jit(solution)/shard_map/ppermute | solution.py:361
  99.6 10.6 %copy-start.11 = (bf16[1,256,512]{2,1,0:T(8,128)(2,1)S(1)}, bf16[1,256,512]{2,1,0:T(8,128)(2,1)}, u32[]{:S(2)}) copy-start(bf16[1,256,512]{2,1,0:T(8,128)(2,1)} %get-tuple-element.29) | copy-start | bytes 786436
  99.6 14.9 %collective-permute-start.14 = (bf16[1,256,512]{2,1,0:T(8,128)(2,1)}, bf16[1,256,512]{2,1,0:T(8,128)(2,1)S(1)}, u32[]{:S(2)}, u32[]{:S(2)}) collective-permute-start(bf16[1,256,512]{2,1,0:T(8,128)(2,1)} %solve.6), channel_id=1, source_target_pairs={{0,4},{1,1},{2,6},{3,3},{4,0},{5,5},{6,2},{7,7},{8,12},{9,9},{10,1... | collective-permute-start | bytes 786440 | tf_op jit(solution)/shard_map/ppermute | solution.py:379
  101.7 12.9 %copy-start.10 = (bf16[1,256,512]{2,1,0:T(8,128)(2,1)S(1)}, bf16[1,256,512]{2,1,0:T(8,128)(2,1)}, u32[]{:S(2)}) copy-start(bf16[1,256,512]{2,1,0:T(8,128)(2,1)} %get-tuple-element.30) | copy-start | bytes 786436
  101.7 13.6 %collective-permute-start.2 = (bf16[1,256,512]{2,1,0:T(8,128)(2,1)S(1)}, bf16[1,256,512]{2,1,0:T(8,128)(2,1)S(1)}, u32[]{:S(2)}, u32[]{:S(2)}) collective-permute-start(bf16[1,256,512]{2,1,0:T(8,128)(2,1)S(1)} %copy-done.12), channel_id=1, source_target_pairs={{0,28},{1,25},{2,30},{3,27},{4,24},{5,29},{6,26},{7,31},{8,20},{9,... | collective-permute-start | bytes 786440 | tf_op jit(solution)/shard_map/ppermute | solution.py:379
  104.6 0.7 copy-start.8
  108.3 15.7 %collective-permute-start.4 = (bf16[1,256,512]{2,1,0:T(8,128)(2,1)}, bf16[1,256,512]{2,1,0:T(8,128)(2,1)S(1)}, u32[]{:S(2)}, u32[]{:S(2)}) collective-permute-start(bf16[1,256,512]{2,1,0:T(8,128)(2,1)} %apply.2), channel_id=1, source_target_pairs={{0,24},{1,29},{2,26},{3,31},{4,28},{5,25},{6,30},{7,27},{8,16},{9,... | collective-permute-start | bytes 786440 | tf_op jit(solution)/shard_map/ppermute | solution.py:379
  110.2 0.8 copy-start.3
  110.2 15.4 %collective-permute-start.7 = (bf16[1,256,512]{2,1,0:T(8,128)(2,1)S(1)}, bf16[1,256,512]{2,1,0:T(8,128)(2,1)S(1)}, u32[]{:S(2)}, u32[]{:S(2)}) collective-permute-start(bf16[1,256,512]{2,1,0:T(8,128)(2,1)S(1)} %copy-done.11), channel_id=1, source_target_pairs={{0,20},{1,17},{2,22},{3,19},{4,16},{5,21},{6,18},{7,23},{8,28},{9,... | collective-permute-start | bytes 786440 | tf_op jit(solution)/shard_map/ppermute | solution.py:379
  114.6 11.1 %collective-permute-start.8 = (bf16[1,256,512]{2,1,0:T(8,128)(2,1)S(1)}, bf16[1,256,512]{2,1,0:T(8,128)(2,1)S(1)}, u32[]{:S(2)}, u32[]{:S(2)}) collective-permute-start(bf16[1,256,512]{2,1,0:T(8,128)(2,1)S(1)} %copy-done.10), channel_id=1, source_target_pairs={{0,12},{1,9},{2,14},{3,11},{4,8},{5,13},{6,10},{7,15},{8,4},{9,1},... | collective-permute-start | bytes 786440 | tf_op jit(solution)/shard_map/ppermute | solution.py:379
  115.3 13.6 %collective-permute-start.10 = (bf16[1,256,512]{2,1,0:T(8,128)(2,1)}, bf16[1,256,512]{2,1,0:T(8,128)(2,1)S(1)}, u32[]{:S(2)}, u32[]{:S(2)}) collective-permute-start(bf16[1,256,512]{2,1,0:T(8,128)(2,1)} %get-tuple-element.32), channel_id=1, source_target_pairs={{0,16},{1,21},{2,18},{3,23},{4,20},{5,17},{6,22},{7,19},{8,24},{9,... | collective-permute-start | bytes 786440 | tf_op jit(solution)/shard_map/ppermute | solution.py:379
  116.2 1.5 %copy-start.9 = (bf16[1,1040,128]{2,1,0:T(8,128)(2,1)}, bf16[1,1040,128]{2,1,0:T(8,128)(2,1)S(1)}, u32[]{:S(2)}) copy-start(bf16[1,1040,128]{2,1,0:T(8,128)(2,1)S(1)} %collective-permute-done.15.total_ref) | copy-start | bytes 798724
  116.2 12.7 %collective-permute-start.11 = (bf16[1,256,512]{2,1,0:T(8,128)(2,1)}, bf16[1,256,512]{2,1,0:T(8,128)(2,1)S(1)}, u32[]{:S(2)}, u32[]{:S(2)}) collective-permute-start(bf16[1,256,512]{2,1,0:T(8,128)(2,1)} %get-tuple-element.33), channel_id=1, source_target_pairs={{0,8},{1,13},{2,10},{3,15},{4,12},{5,9},{6,14},{7,11},{8,0},{9,5},... | collective-permute-start | bytes 786440 | tf_op jit(solution)/shard_map/ppermute | solution.py:379
  124.0 5.2 %collective-permute-start.16 = (bf16[1,256,512]{2,1,0:T(8,128)(2,1)}, bf16[1,256,512]{2,1,0:T(8,128)(2,1)S(1)}, u32[]{:S(2)}, u32[]{:S(2)}) collective-permute-start(bf16[1,256,512]{2,1,0:T(8,128)(2,1)} %solve.7), channel_id=1, source_target_pairs={{0,0},{1,5},{2,2},{3,7},{4,4},{5,1},{6,6},{7,3},{8,8},{9,13},{10,1... | collective-permute-start | bytes 786440 | tf_op jit(solution)/shard_map/ppermute | solution.py:379
  129.3 1.3 %copy-start = (bf16[8,256,512]{2,1,0:T(8,128)(2,1)}, bf16[8,256,512]{2,1,0:T(8,128)(2,1)S(1)}, u32[]{:S(2)}) copy-start(bf16[8,256,512]{2,1,0:T(8,128)(2,1)S(1)} %constant_dynamic-update-slice_fusion.1) | copy-start | bytes 6291460

commit v3 on v2

--- a/solution.py
+++ b/solution.py
@@ -179,14 +179,13 @@
 
 
 def solve_kernel(plan, offset, number, dest_ref, total_ref, state_ref, *refs):
-    out_refs, (total_buf, state_buf, sem, state_sem) = refs[:-4], refs[-4:]
+    out_refs, (state_buf, state_sem) = refs[:-2], refs[-2:]
     members = state_buf.shape[2]
     blocks = members // LANES
-    fetch = [pltpu.make_async_copy(total_ref.at[k], total_buf.at[k], sem.at[k]) for k in range(number)]
     picked = [pick_group(dest_ref, plan, offset + k) for k in range(number)]
     states = [
         pltpu.make_async_copy(state_ref.at[g], state_buf.at[k], state_sem.at[k]) for k, g in enumerate(picked)]
-    for copy in fetch + states:
+    for copy in states:
         copy.start()
     big_row = lax.broadcasted_iota(jnp.int32, (members, members), 0)
     big_col = lax.broadcasted_iota(jnp.int32, (members, members), 1)
@@ -198,8 +197,7 @@
 
     roots, scales, rhs = [], [], []
     for k in range(number):
-        fetch[k].wait()
-        gram, tail = load_packed(total_buf, k, members)
+        gram, tail = load_packed(total_ref, k, members)
         matrix = gram + jnp.where(eye, members - 1.0, 0.0)
         square = jnp.sum(matrix * matrix, axis=0, keepdims=True)
         scale = jnp.sqrt(jnp.sum(square, axis=1, keepdims=True))
@@ -244,18 +242,16 @@
 
 
 def apply_kernel(plan, offset, number, dest_ref, packed_ref, state_ref, *refs):
-    out_refs, (packed_buf, state_buf, sem, state_sem) = refs[:-4], refs[-4:]
+    out_refs, (state_buf, state_sem) = refs[:-2], refs[-2:]
     members = state_buf.shape[2]
     blocks = members // LANES
-    fetch = [pltpu.make_async_copy(packed_ref.at[k], packed_buf.at[k], sem.at[k]) for k in range(number)]
     picked = [pick_group(dest_ref, plan, offset + k) for k in range(number)]
     states = [
         pltpu.make_async_copy(state_ref.at[g], state_buf.at[k], state_sem.at[k]) for k, g in enumerate(picked)]
-    for copy in fetch + states:
+    for copy in states:
         copy.start()
     for k in range(number):
-        fetch[k].wait()
-        inverse, tail = load_packed(packed_buf, k, members)
+        inverse, tail = load_packed(packed_ref, k, members)
         spread = tail[12:13, :1] + tail[13:14, :1] + tail[14:15, :1]
         means = tail[:8] + pltpu.roll(tail[:8], 4, 0)
         column = jnp.concatenate(
@@ -276,13 +272,12 @@
         out_shape=[jax.ShapeDtypeStruct((1, here, members), BF16)] * number + packed,
         in_specs=[
             pl.BlockSpec(memory_space=pltpu.SMEM),
-            pl.BlockSpec(memory_space=pl.ANY),
+            pl.BlockSpec(memory_space=pltpu.VMEM),
             pl.BlockSpec(memory_space=pl.ANY),
         ],
         out_specs=[pl.BlockSpec(memory_space=pltpu.VMEM)] * (number + len(packed)),
         scratch_shapes=[
-            pltpu.VMEM((number, rows, lanes), BF16), pltpu.VMEM((number, here, members), BF16),
-            pltpu.SemaphoreType.DMA((number,)), pltpu.SemaphoreType.DMA((number,))],
+            pltpu.VMEM((number, here, members), BF16), pltpu.SemaphoreType.DMA((number,))],
         cost_estimate=pl.CostEstimate(
             flops=number * products * 2 * members ** 3, transcendentals=0,
             bytes_accessed=number * (2 * rows * lanes + 4 * here * members)),

time: 132 us -> 131 us (level)
  Pallas kernels: 47.1 us -> 44.8 us
    pallas_call x6, Pallas kernels: 35.2 us -> 32.9 us  [solve_call(): pl.pallas_call(functools.partial(kernel, plan, offset, number), out_shape...]
  transfers between devices with their start and end apart: 17 -> 17, of which waited for: 4 -> 5; matrix products, arithmetic and copies ran while one was open for 1% -> 1% of each run, Pallas kernels for 32% -> 31%
where the time goes in v3:
time: 131 us
  waiting for transfers between devices  52.6 us (40%)
  Pallas kernels  44.8 us (34%)
  starting transfers between devices  27.5 us (21%)
  local copies, waits for them, and re-layouts  4.62 us (4%)
    pallas_call x6, Pallas kernels, solve_call(): pl.pallas_call(functools.partial(kernel, plan, offset, number), out_shape...  32.9 us
    ppermute x3, waiting for transfers between devices, body(): arrived = lax.ppermute(mine, 'own', cross)  31.5 us
    ppermute x3, waiting for transfers between devices, body(): arrived = lax.ppermute(sends[chunk], 'own', pair)  17.2 us
    ppermute x8, starting transfers between devices, body(): arrivals.append(lax.ppermute(done, ('grp', 'own'), pairs))  12.9 us
    pallas_call x3, Pallas kernels, gram_call(): pl.pallas_call(functools.partial(gram_kernel, plan, wanted), out_shape=[j...  11.9 us
    ppermute x3, starting transfers between devices, body(): arrived = lax.ppermute(sends[chunk], 'own', pair)  5.2 us
    ppermute x3, starting transfers between devices, body(): arrived = lax.ppermute(mine, 'own', cross)  4.76 us
    ppermute x8, waiting for transfers between devices, body(): arrivals.append(lax.ppermute(done, ('grp', 'own'), pairs))  3.88 us
  transfers between devices with their start and end apart: 17, of which 5 were waited for; matrix products, arithmetic and copies ran while one was open for 1% of the time, Pallas kernels for 31%

profile of v3, /device:TPU:0, one launch (start us, length us, event | category | flops | bytes accessed | tf_op | source)
XLA Modules:
  0.0 130.7 jit_solution(7118274236398545750)
XLA Ops:
  0.0 4.6 %gram.5 = (bf16[2,1040,128]{2,1,0:T(8,128)(2,1)}, bf16[1,1040,128]{2,1,0:T(8,128)(2,1)}, bf16[1,1040,128]{2,1,0:T(8,128)(2,1)}) custom-call(s32[64]{0:T(128)} %dest_ref.17, s32[8]{0:T(128)} %bitcast.1, bf16[8,512,512]{2,1,0:T(8,128)(2,1)} %obs_ref.5, bf16[8,512]{1,0:T(8,128)(2,1)} %weight_ref.5, bf16[8,512]{1,0:T(8,128)(2,1)} %innov_ref.5), custom_call_target="tpu_custom_call" | custom-call | flops 1073741824 | bytes 3162112 | tf_op jit(solution)/shard_map/gram/pallas_call | solution.py:145
  4.6 3.1 %collective-permute-start.12 = (bf16[1,1040,128]{2,1,0:T(8,128)(2,1)}, bf16[1,1040,128]{2,1,0:T(8,128)(2,1)S(1)}, u32[]{:S(2)}, u32[]{:S(2)}) collective-permute-start(bf16[1,1040,128]{2,1,0:T(8,128)(2,1)} %get-tuple-element.35), channel_id=1, source_target_pairs={{0,1},{1,0},{2,3},{3,2},{4,5},{5,4},{6,7},{7,6},{8,9},{9,8},{10,11... | collective-permute-start | bytes 798728 | tf_op jit(solution)/shard_map/ppermute | solution.py:346
  7.7 4.1 %gram.3 = (bf16[1,1040,128]{2,1,0:T(8,128)(2,1)}, bf16[2,1040,128]{2,1,0:T(8,128)(2,1)}) custom-call(s32[64]{0:T(128)} %dest_ref.17, s32[8]{0:T(128)} %bitcast.2, bf16[8,512,512]{2,1,0:T(8,128)(2,1)} %obs_ref.5, bf16[8,512]{1,0:T(8,128)(2,1)} %weight_ref.5, bf16[8,512]{1,0:T(8,128)(2,1)} %innov_ref.5), custom_call_target="tpu_custom_call" | custom-call | flops 805306368 | bytes 2371584 | tf_op jit(solution)/shard_map/gram/pallas_call | solution.py:145
  11.9 3.2 %gram.4 = bf16[1,1040,128]{2,1,0:T(8,128)(2,1)} custom-call(s32[64]{0:T(128)} %dest_ref.17, s32[8]{0:T(128)} %bitcast.3, bf16[8,512,512]{2,1,0:T(8,128)(2,1)} %obs_ref.5, bf16[8,512]{1,0:T(8,128)(2,1)} %weight_ref.5, bf16[8,512]{1,0:T(8,128)(2,1)} %innov_ref.5), custom_call_target="tpu_custom_call" | custom-call | flops 268435456 | bytes 790528 | tf_op jit(solution)/shard_map/gram/pallas_call | solution.py:145
  15.2 2.0 %collective-permute-start = (bf16[1,1040,128]{2,1,0:T(8,128)(2,1)}, bf16[1,1040,128]{2,1,0:T(8,128)(2,1)S(1)}, u32[]{:S(2)}, u32[]{:S(2)}) collective-permute-start(bf16[1,1040,128]{2,1,0:T(8,128)(2,1)} %gram.4), channel_id=1, source_target_pairs={{0,1},{1,0},{2,3},{3,2},{4,5},{5,4},{6,7},{7,6},{8,9},{9,8},{10,11... | collective-permute-start | bytes 798728 | tf_op jit(solution)/shard_map/ppermute | solution.py:346
  17.3 2.6 %collective-permute-start.13 = (bf16[1,1040,128]{2,1,0:T(8,128)(2,1)S(1)}, bf16[1,1040,128]{2,1,0:T(8,128)(2,1)S(1)}, u32[]{:S(2)}, u32[]{:S(2)}) collective-permute-start(bf16[1,1040,128]{2,1,0:T(8,128)(2,1)S(1)} %constant_dynamic-update-slice_fusion.9), channel_id=1, source_target_pairs={{0,2},{1,3},{2,0},{3,1},{4,6},{5,7},{6,4},{7,5},{8,10},{9,11},{10,... | collective-permute-start | bytes 798728 | tf_op jit(solution)/shard_map/ppermute | solution.py:349
  19.9 17.2 %collective-permute-done = bf16[1,1040,128]{2,1,0:T(8,128)(2,1)S(1)} collective-permute-done((bf16[1,1040,128]{2,1,0:T(8,128)(2,1)}, bf16[1,1040,128]{2,1,0:T(8,128)(2,1)S(1)}, u32[]{:S(2)}, u32[]{:S(2)}) %collective-permute-start) | collective-permute-done | bytes 266272 | tf_op jit(solution)/shard_map/ppermute | solution.py:346
  37.2 2.0 %collective-permute-start.1 = (bf16[1,1040,128]{2,1,0:T(8,128)(2,1)S(1)}, bf16[1,1040,128]{2,1,0:T(8,128)(2,1)S(1)}, u32[]{:S(2)}, u32[]{:S(2)}) collective-permute-start(bf16[1,1040,128]{2,1,0:T(8,128)(2,1)S(1)} %constant_dynamic-update-slice_fusion.12), channel_id=1, source_target_pairs={{0,2},{1,3},{2,0},{3,1},{4,6},{5,7},{6,4},{7,5},{8,10},{9,11},{10,... | collective-permute-start | bytes 798728 | tf_op jit(solution)/shard_map/ppermute | solution.py:349
  39.4 2.4 %collective-permute-start.15 = (bf16[1,1040,128]{2,1,0:T(8,128)(2,1)S(1)}, bf16[1,1040,128]{2,1,0:T(8,128)(2,1)S(1)}, u32[]{:S(2)}, u32[]{:S(2)}) collective-permute-start(bf16[1,1040,128]{2,1,0:T(8,128)(2,1)S(1)} %constant_dynamic-update-slice_fusion.8.total_ref), channel_id=1, source_target_pairs={{0,1},{1,0},{2,3},{3,2},{4,5},{5,4},{6,7},{7,6},{8,9},{9,8},{10,11... | collective-permute-start | bytes 798728 | tf_op jit(solution)/shard_map/ppermute | solution.py:353
  42.1 12.0 %collective-permute-done.1 = bf16[1,1040,128]{2,1,0:T(8,128)(2,1)S(1)} collective-permute-done((bf16[1,1040,128]{2,1,0:T(8,128)(2,1)S(1)}, bf16[1,1040,128]{2,1,0:T(8,128)(2,1)S(1)}, u32[]{:S(2)}, u32[]{:S(2)}) %collective-permute-start.1) | collective-permute-done | bytes 266272 | tf_op jit(solution)/shard_map/ppermute | solution.py:349
  54.2 19.5 %collective-permute-done.6 = bf16[2,1040,128]{2,1,0:T(8,128)(2,1)S(1)} collective-permute-done((bf16[2,1040,128]{2,1,0:T(8,128)(2,1)S(1)}, bf16[2,1040,128]{2,1,0:T(8,128)(2,1)S(1)}, u32[]{:S(2)}, u32[]{:S(2)}) %collective-permute-start.6) | collective-permute-done | bytes 532512 | tf_op jit(solution)/shard_map/ppermute | solution.py:349
  74.0 0.8 copy-done.2
  74.8 9.2 %solve.5 = (bf16[1,256,512]{2,1,0:T(8,128)(2,1)}, bf16[1,256,512]{2,1,0:T(8,128)(2,1)}, bf16[2,1040,128]{2,1,0:T(8,128)(2,1)}) custom-call(s32[64]{0:T(128)} %dest_ref.17, bf16[2,1040,128]{2,1,0:T(8,128)(2,1)} %copy-done.2, bf16[8,256,512]{2,1,0:T(8,128)(2,1)} %state_ref.11), custom_call_target="tpu_custom_call" | custom-call | flops 4831838208 | bytes 1581056 | tf_op jit(solution)/shard_map/solve/pallas_call | solution.py:270
  84.0 0.4 collective-permute-start.9
  84.3 5.7 %solve.4 = (bf16[1,256,512]{2,1,0:T(8,128)(2,1)}, bf16[1,1040,128]{2,1,0:T(8,128)(2,1)}) custom-call(s32[64]{0:T(128)} %dest_ref.17, bf16[1,1040,128]{2,1,0:T(8,128)(2,1)} %copy-done.7, bf16[8,256,512]{2,1,0:T(8,128)(2,1)} %state_ref.11), custom_call_target="tpu_custom_call" | custom-call | flops 2415919104 | bytes 790528 | tf_op jit(solution)/shard_map/solve/pallas_call | solution.py:270
  90.1 1.8 %collective-permute-start.3 = (bf16[1,1040,128]{2,1,0:T(8,128)(2,1)}, bf16[1,1040,128]{2,1,0:T(8,128)(2,1)S(1)}, u32[]{:S(2)}, u32[]{:S(2)}) collective-permute-start(bf16[1,1040,128]{2,1,0:T(8,128)(2,1)} %get-tuple-element.26), channel_id=1, source_target_pairs={{0,1},{1,0},{2,3},{3,2},{4,5},{5,4},{6,7},{7,6},{8,9},{9,8},{10,11... | collective-permute-start | bytes 798728 | tf_op jit(solution)/shard_map/ppermute | solution.py:356
  91.9 5.7 %solve.6 = bf16[1,256,512]{2,1,0:T(8,128)(2,1)} custom-call(s32[64]{0:T(128)} %dest_ref.17, bf16[1,1040,128]{2,1,0:T(8,128)(2,1)} %copy-done.6, bf16[8,256,512]{2,1,0:T(8,128)(2,1)} %state_ref.11), custom_call_target="tpu_custom_call" | custom-call | flops 2415919104 | bytes 790528 | tf_op jit(solution)/shard_map/solve/pallas_call | solution.py:270
  97.6 2.1 %collective-permute-start.14 = (bf16[1,256,512]{2,1,0:T(8,128)(2,1)}, bf16[1,256,512]{2,1,0:T(8,128)(2,1)S(1)}, u32[]{:S(2)}, u32[]{:S(2)}) collective-permute-start(bf16[1,256,512]{2,1,0:T(8,128)(2,1)} %solve.6), channel_id=1, source_target_pairs={{0,4},{1,1},{2,6},{3,3},{4,0},{5,5},{6,2},{7,7},{8,12},{9,9},{10,1... | collective-permute-start | bytes 786440 | tf_op jit(solution)/shard_map/ppermute | solution.py:374
  99.7 3.0 %collective-permute-start.2 = (bf16[1,256,512]{2,1,0:T(8,128)(2,1)S(1)}, bf16[1,256,512]{2,1,0:T(8,128)(2,1)S(1)}, u32[]{:S(2)}, u32[]{:S(2)}) collective-permute-start(bf16[1,256,512]{2,1,0:T(8,128)(2,1)S(1)} %copy-done.12), channel_id=1, source_target_pairs={{0,28},{1,25},{2,30},{3,27},{4,24},{5,29},{6,26},{7,31},{8,20},{9,... | collective-permute-start | bytes 786440 | tf_op jit(solution)/shard_map/ppermute | solution.py:374
  102.6 0.7 copy-done.8
  103.3 3.1 %apply.2 = bf16[1,256,512]{2,1,0:T(8,128)(2,1)} custom-call(s32[64]{0:T(128)} %dest_ref.17, bf16[1,1040,128]{2,1,0:T(8,128)(2,1)} %copy-done.8, bf16[8,256,512]{2,1,0:T(8,128)(2,1)} %state_ref.11), custom_call_target="tpu_custom_call" | custom-call | flops 268435456 | bytes 790528 | tf_op jit(solution)/shard_map/apply/pallas_call | solution.py:270
  106.4 3.2 %collective-permute-start.4 = (bf16[1,256,512]{2,1,0:T(8,128)(2,1)}, bf16[1,256,512]{2,1,0:T(8,128)(2,1)S(1)}, u32[]{:S(2)}, u32[]{:S(2)}) collective-permute-start(bf16[1,256,512]{2,1,0:T(8,128)(2,1)} %apply.2), channel_id=1, source_target_pairs={{0,24},{1,29},{2,26},{3,31},{4,28},{5,25},{6,30},{7,27},{8,16},{9,... | collective-permute-start | bytes 786440 | tf_op jit(solution)/shard_map/ppermute | solution.py:374
  109.7 0.7 copy-done.3
  110.4 3.6 %apply.3 = (bf16[1,256,512]{2,1,0:T(8,128)(2,1)}, bf16[1,256,512]{2,1,0:T(8,128)(2,1)}) custom-call(s32[64]{0:T(128)} %dest_ref.17, bf16[2,1040,128]{2,1,0:T(8,128)(2,1)} %copy-done.3, bf16[8,256,512]{2,1,0:T(8,128)(2,1)} %state_ref.11), custom_call_target="tpu_custom_call" | custom-call | flops 536870912 | bytes 1581056 | tf_op jit(solution)/shard_map/apply/pallas_call | solution.py:270
  114.1 1.5 %collective-permute-start.10 = (bf16[1,256,512]{2,1,0:T(8,128)(2,1)}, bf16[1,256,512]{2,1,0:T(8,128)(2,1)S(1)}, u32[]{:S(2)}, u32[]{:S(2)}) collective-permute-start(bf16[1,256,512]{2,1,0:T(8,128)(2,1)} %get-tuple-element.32), channel_id=1, source_target_pairs={{0,16},{1,21},{2,18},{3,23},{4,20},{5,17},{6,22},{7,19},{8,24},{9,... | collective-permute-start | bytes 786440 | tf_op jit(solution)/shard_map/ppermute | solution.py:374
  115.6 1.5 %collective-permute-start.11 = (bf16[1,256,512]{2,1,0:T(8,128)(2,1)}, bf16[1,256,512]{2,1,0:T(8,128)(2,1)S(1)}, u32[]{:S(2)}, u32[]{:S(2)}) collective-permute-start(bf16[1,256,512]{2,1,0:T(8,128)(2,1)} %get-tuple-element.33), channel_id=1, source_target_pairs={{0,8},{1,13},{2,10},{3,15},{4,12},{5,9},{6,14},{7,11},{8,0},{9,5},... | collective-permute-start | bytes 786440 | tf_op jit(solution)/shard_map/ppermute | solution.py:374
  117.1 5.7 %solve.7 = bf16[1,256,512]{2,1,0:T(8,128)(2,1)} custom-call(s32[64]{0:T(128)} %dest_ref.17, bf16[1,1040,128]{2,1,0:T(8,128)(2,1)} %copy-done.9, bf16[8,256,512]{2,1,0:T(8,128)(2,1)} %state_ref.11), custom_call_target="tpu_custom_call" | custom-call | flops 2415919104 | bytes 790528 | tf_op jit(solution)/shard_map/solve/pallas_call | solution.py:270
  122.8 1.6 %collective-permute-start.16 = (bf16[1,256,512]{2,1,0:T(8,128)(2,1)}, bf16[1,256,512]{2,1,0:T(8,128)(2,1)S(1)}, u32[]{:S(2)}, u32[]{:S(2)}) collective-permute-start(bf16[1,256,512]{2,1,0:T(8,128)(2,1)} %solve.7), channel_id=1, source_target_pairs={{0,0},{1,5},{2,2},{3,7},{4,4},{5,1},{6,6},{7,3},{8,8},{9,13},{10,1... | collective-permute-start | bytes 786440 | tf_op jit(solution)/shard_map/ppermute | solution.py:374
  124.4 2.6 %collective-permute-done.10 = bf16[1,256,512]{2,1,0:T(8,128)(2,1)S(1)} collective-permute-done((bf16[1,256,512]{2,1,0:T(8,128)(2,1)}, bf16[1,256,512]{2,1,0:T(8,128)(2,1)S(1)}, u32[]{:S(2)}, u32[]{:S(2)}) %collective-permute-start.10) | collective-permute-done | bytes 262176 | tf_op jit(solution)/shard_map/ppermute | solution.py:374
  127.0 1.3 %collective-permute-done.11 = bf16[1,256,512]{2,1,0:T(8,128)(2,1)S(1)} collective-permute-done((bf16[1,256,512]{2,1,0:T(8,128)(2,1)}, bf16[1,256,512]{2,1,0:T(8,128)(2,1)S(1)}, u32[]{:S(2)}, u32[]{:S(2)}) %collective-permute-start.11) | collective-permute-done | bytes 262176 | tf_op jit(solution)/shard_map/ppermute | solution.py:374
  128.7 1.3 copy-done
  130.0 0.7 constant_dynamic-update-slice_fusion
  (70 shorter events, 1.5 us)
Async XLA Ops:
  4.6 12.6 %collective-permute-start.12 = (bf16[1,1040,128]{2,1,0:T(8,128)(2,1)}, bf16[1,1040,128]{2,1,0:T(8,128)(2,1)S(1)}, u32[]{:S(2)}, u32[]{:S(2)}) collective-permute-start(bf16[1,1040,128]{2,1,0:T(8,128)(2,1)} %get-tuple-element.35), channel_id=1, source_target_pairs={{0,1},{1,0},{2,3},{3,2},{4,5},{5,4},{6,7},{7,6},{8,9},{9,8},{10,11... | collective-permute-start | bytes 798728 | tf_op jit(solution)/shard_map/ppermute | solution.py:346
  11.8 5.3 %copy-start.5 = (bf16[1,1040,128]{2,1,0:T(8,128)(2,1)S(1)}, bf16[1,1040,128]{2,1,0:T(8,128)(2,1)}, u32[]{:S(2)}) copy-start(bf16[1,1040,128]{2,1,0:T(8,128)(2,1)} %get-tuple-element.34) | copy-start | bytes 798724
  11.8 25.3 %copy-start.4 = (bf16[1,1040,128]{2,1,0:T(8,128)(2,1)S(1)}, bf16[1,1040,128]{2,1,0:T(8,128)(2,1)}, u32[]{:S(2)}) copy-start(bf16[1,1040,128]{2,1,0:T(8,128)(2,1)} %get-tuple-element.24) | copy-start | bytes 798724
  11.8 30.0 %collective-permute-start.5 = (bf16[2,1040,128]{2,1,0:T(8,128)(2,1)}, bf16[2,1040,128]{2,1,0:T(8,128)(2,1)S(1)}, u32[]{:S(2)}, u32[]{:S(2)}) collective-permute-start(bf16[2,1040,128]{2,1,0:T(8,128)(2,1)} %get-tuple-element.28), channel_id=1, source_target_pairs={{0,1},{1,0},{2,3},{3,2},{4,5},{5,4},{6,7},{7,6},{8,9},{9,8},{10,11... | collective-permute-start | bytes 1597448 | tf_op jit(solution)/shard_map/ppermute | solution.py:346
  15.2 26.7 %copy-start.1 = (bf16[2,1040,128]{2,1,0:T(8,128)(2,1)S(1)}, bf16[2,1040,128]{2,1,0:T(8,128)(2,1)}, u32[]{:S(2)}) copy-start(bf16[2,1040,128]{2,1,0:T(8,128)(2,1)} %get-tuple-element.27) | copy-start | bytes 1597444
  15.2 21.9 %collective-permute-start = (bf16[1,1040,128]{2,1,0:T(8,128)(2,1)}, bf16[1,1040,128]{2,1,0:T(8,128)(2,1)S(1)}, u32[]{:S(2)}, u32[]{:S(2)}) collective-permute-start(bf16[1,1040,128]{2,1,0:T(8,128)(2,1)} %gram.4), channel_id=1, source_target_pairs={{0,1},{1,0},{2,3},{3,2},{4,5},{5,4},{6,7},{7,6},{8,9},{9,8},{10,11... | collective-permute-start | bytes 798728 | tf_op jit(solution)/shard_map/ppermute | solution.py:346
  17.3 22.0 %collective-permute-start.13 = (bf16[1,1040,128]{2,1,0:T(8,128)(2,1)S(1)}, bf16[1,1040,128]{2,1,0:T(8,128)(2,1)S(1)}, u32[]{:S(2)}, u32[]{:S(2)}) collective-permute-start(bf16[1,1040,128]{2,1,0:T(8,128)(2,1)S(1)} %constant_dynamic-update-slice_fusion.9), channel_id=1, source_target_pairs={{0,2},{1,3},{2,0},{3,1},{4,6},{5,7},{6,4},{7,5},{8,10},{9,11},{10,... | collective-permute-start | bytes 798728 | tf_op jit(solution)/shard_map/ppermute | solution.py:349
  37.2 16.9 %collective-permute-start.1 = (bf16[1,1040,128]{2,1,0:T(8,128)(2,1)S(1)}, bf16[1,1040,128]{2,1,0:T(8,128)(2,1)S(1)}, u32[]{:S(2)}, u32[]{:S(2)}) collective-permute-start(bf16[1,1040,128]{2,1,0:T(8,128)(2,1)S(1)} %constant_dynamic-update-slice_fusion.12), channel_id=1, source_target_pairs={{0,2},{1,3},{2,0},{3,1},{4,6},{5,7},{6,4},{7,5},{8,10},{9,11},{10,... | collective-permute-start | bytes 798728 | tf_op jit(solution)/shard_map/ppermute | solution.py:349
  39.4 44.6 %copy-start.6 = (bf16[1,1040,128]{2,1,0:T(8,128)(2,1)}, bf16[1,1040,128]{2,1,0:T(8,128)(2,1)S(1)}, u32[]{:S(2)}) copy-start(bf16[1,1040,128]{2,1,0:T(8,128)(2,1)S(1)} %constant_dynamic-update-slice_fusion.8.total_ref) | copy-start | bytes 798724
  39.4 76.2 %collective-permute-start.15 = (bf16[1,1040,128]{2,1,0:T(8,128)(2,1)S(1)}, bf16[1,1040,128]{2,1,0:T(8,128)(2,1)S(1)}, u32[]{:S(2)}, u32[]{:S(2)}) collective-permute-start(bf16[1,1040,128]{2,1,0:T(8,128)(2,1)S(1)} %constant_dynamic-update-slice_fusion.8.total_ref), channel_id=1, source_target_pairs={{0,1},{1,0},{2,3},{3,2},{4,5},{5,4},{6,7},{7,6},{8,9},{9,8},{10,11... | collective-permute-start | bytes 798728 | tf_op jit(solution)/shard_map/ppermute | solution.py:353
  42.0 31.8 %collective-permute-start.6 = (bf16[2,1040,128]{2,1,0:T(8,128)(2,1)S(1)}, bf16[2,1040,128]{2,1,0:T(8,128)(2,1)S(1)}, u32[]{:S(2)}, u32[]{:S(2)}) collective-permute-start(bf16[2,1040,128]{2,1,0:T(8,128)(2,1)S(1)} %constant_dynamic-update-slice_fusion.10), channel_id=1, source_target_pairs={{0,2},{1,3},{2,0},{3,1},{4,6},{5,7},{6,4},{7,5},{8,10},{9,11},{10,... | collective-permute-start | bytes 1597448 | tf_op jit(solution)/shard_map/ppermute | solution.py:349
  54.2 29.7 %copy-start.7 = (bf16[1,1040,128]{2,1,0:T(8,128)(2,1)}, bf16[1,1040,128]{2,1,0:T(8,128)(2,1)S(1)}, u32[]{:S(2)}) copy-start(bf16[1,1040,128]{2,1,0:T(8,128)(2,1)S(1)} %constant_dynamic-update-slice_fusion.11.total_ref) | copy-start | bytes 798724
  74.0 0.8 copy-start.2
  84.0 25.6 %collective-permute-start.9 = (bf16[2,1040,128]{2,1,0:T(8,128)(2,1)}, bf16[2,1040,128]{2,1,0:T(8,128)(2,1)S(1)}, u32[]{:S(2)}, u32[]{:S(2)}) collective-permute-start(bf16[2,1040,128]{2,1,0:T(8,128)(2,1)} %get-tuple-element.31), channel_id=1, source_target_pairs={{0,1},{1,0},{2,3},{3,2},{4,5},{5,4},{6,7},{7,6},{8,9},{9,8},{10,11... | collective-permute-start | bytes 1597448 | tf_op jit(solution)/shard_map/ppermute | solution.py:356
  90.1 9.6 %copy-start.12 = (bf16[1,256,512]{2,1,0:T(8,128)(2,1)S(1)}, bf16[1,256,512]{2,1,0:T(8,128)(2,1)}, u32[]{:S(2)}) copy-start(bf16[1,256,512]{2,1,0:T(8,128)(2,1)} %get-tuple-element.25) | copy-start | bytes 786436
  90.1 12.5 %collective-permute-start.3 = (bf16[1,1040,128]{2,1,0:T(8,128)(2,1)}, bf16[1,1040,128]{2,1,0:T(8,128)(2,1)S(1)}, u32[]{:S(2)}, u32[]{:S(2)}) collective-permute-start(bf16[1,1040,128]{2,1,0:T(8,128)(2,1)} %get-tuple-element.26), channel_id=1, source_target_pairs={{0,1},{1,0},{2,3},{3,2},{4,5},{5,4},{6,7},{7,6},{8,9},{9,8},{10,11... | collective-permute-start | bytes 798728 | tf_op jit(solution)/shard_map/ppermute | solution.py:356
  97.6 12.0 %copy-start.11 = (bf16[1,256,512]{2,1,0:T(8,128)(2,1)S(1)}, bf16[1,256,512]{2,1,0:T(8,128)(2,1)}, u32[]{:S(2)}) copy-start(bf16[1,256,512]{2,1,0:T(8,128)(2,1)} %get-tuple-element.29) | copy-start | bytes 786436
  97.6 16.4 %collective-permute-start.14 = (bf16[1,256,512]{2,1,0:T(8,128)(2,1)}, bf16[1,256,512]{2,1,0:T(8,128)(2,1)S(1)}, u32[]{:S(2)}, u32[]{:S(2)}) collective-permute-start(bf16[1,256,512]{2,1,0:T(8,128)(2,1)} %solve.6), channel_id=1, source_target_pairs={{0,4},{1,1},{2,6},{3,3},{4,0},{5,5},{6,2},{7,7},{8,12},{9,9},{10,1... | collective-permute-start | bytes 786440 | tf_op jit(solution)/shard_map/ppermute | solution.py:374
  99.7 14.3 %copy-start.10 = (bf16[1,256,512]{2,1,0:T(8,128)(2,1)S(1)}, bf16[1,256,512]{2,1,0:T(8,128)(2,1)}, u32[]{:S(2)}) copy-start(bf16[1,256,512]{2,1,0:T(8,128)(2,1)} %get-tuple-element.30) | copy-start | bytes 786436
  99.7 14.4 %collective-permute-start.2 = (bf16[1,256,512]{2,1,0:T(8,128)(2,1)S(1)}, bf16[1,256,512]{2,1,0:T(8,128)(2,1)S(1)}, u32[]{:S(2)}, u32[]{:S(2)}) collective-permute-start(bf16[1,256,512]{2,1,0:T(8,128)(2,1)S(1)} %copy-done.12), channel_id=1, source_target_pairs={{0,28},{1,25},{2,30},{3,27},{4,24},{5,29},{6,26},{7,31},{8,20},{9,... | collective-permute-start | bytes 786440 | tf_op jit(solution)/shard_map/ppermute | solution.py:374
  102.6 0.7 copy-start.8
  106.4 16.4 %collective-permute-start.4 = (bf16[1,256,512]{2,1,0:T(8,128)(2,1)}, bf16[1,256,512]{2,1,0:T(8,128)(2,1)S(1)}, u32[]{:S(2)}, u32[]{:S(2)}) collective-permute-start(bf16[1,256,512]{2,1,0:T(8,128)(2,1)} %apply.2), channel_id=1, source_target_pairs={{0,24},{1,29},{2,26},{3,31},{4,28},{5,25},{6,30},{7,27},{8,16},{9,... | collective-permute-start | bytes 786440 | tf_op jit(solution)/shard_map/ppermute | solution.py:374
  109.6 0.8 copy-start.3
  109.6 14.8 %collective-permute-start.7 = (bf16[1,256,512]{2,1,0:T(8,128)(2,1)S(1)}, bf16[1,256,512]{2,1,0:T(8,128)(2,1)S(1)}, u32[]{:S(2)}, u32[]{:S(2)}) collective-permute-start(bf16[1,256,512]{2,1,0:T(8,128)(2,1)S(1)} %copy-done.11), channel_id=1, source_target_pairs={{0,20},{1,17},{2,22},{3,19},{4,16},{5,21},{6,18},{7,23},{8,28},{9,... | collective-permute-start | bytes 786440 | tf_op jit(solution)/shard_map/ppermute | solution.py:374
  114.0 10.4 %collective-permute-start.8 = (bf16[1,256,512]{2,1,0:T(8,128)(2,1)S(1)}, bf16[1,256,512]{2,1,0:T(8,128)(2,1)S(1)}, u32[]{:S(2)}, u32[]{:S(2)}) collective-permute-start(bf16[1,256,512]{2,1,0:T(8,128)(2,1)S(1)} %copy-done.10), channel_id=1, source_target_pairs={{0,12},{1,9},{2,14},{3,11},{4,8},{5,13},{6,10},{7,15},{8,4},{9,1},... | collective-permute-start | bytes 786440 | tf_op jit(solution)/shard_map/ppermute | solution.py:374
  114.1 12.9 %collective-permute-start.10 = (bf16[1,256,512]{2,1,0:T(8,128)(2,1)}, bf16[1,256,512]{2,1,0:T(8,128)(2,1)S(1)}, u32[]{:S(2)}, u32[]{:S(2)}) collective-permute-start(bf16[1,256,512]{2,1,0:T(8,128)(2,1)} %get-tuple-element.32), channel_id=1, source_target_pairs={{0,16},{1,21},{2,18},{3,23},{4,20},{5,17},{6,22},{7,19},{8,24},{9,... | collective-permute-start | bytes 786440 | tf_op jit(solution)/shard_map/ppermute | solution.py:374
  115.6 1.5 %copy-start.9 = (bf16[1,1040,128]{2,1,0:T(8,128)(2,1)}, bf16[1,1040,128]{2,1,0:T(8,128)(2,1)S(1)}, u32[]{:S(2)}) copy-start(bf16[1,1040,128]{2,1,0:T(8,128)(2,1)S(1)} %collective-permute-done.15.total_ref) | copy-start | bytes 798724
  115.6 12.7 %collective-permute-start.11 = (bf16[1,256,512]{2,1,0:T(8,128)(2,1)}, bf16[1,256,512]{2,1,0:T(8,128)(2,1)S(1)}, u32[]{:S(2)}, u32[]{:S(2)}) collective-permute-start(bf16[1,256,512]{2,1,0:T(8,128)(2,1)} %get-tuple-element.33), channel_id=1, source_target_pairs={{0,8},{1,13},{2,10},{3,15},{4,12},{5,9},{6,14},{7,11},{8,0},{9,5},... | collective-permute-start | bytes 786440 | tf_op jit(solution)/shard_map/ppermute | solution.py:374
  122.8 5.9 %collective-permute-start.16 = (bf16[1,256,512]{2,1,0:T(8,128)(2,1)}, bf16[1,256,512]{2,1,0:T(8,128)(2,1)S(1)}, u32[]{:S(2)}, u32[]{:S(2)}) collective-permute-start(bf16[1,256,512]{2,1,0:T(8,128)(2,1)} %solve.7), channel_id=1, source_target_pairs={{0,0},{1,5},{2,2},{3,7},{4,4},{5,1},{6,6},{7,3},{8,8},{9,13},{10,1... | collective-permute-start | bytes 786440 | tf_op jit(solution)/shard_map/ppermute | solution.py:374
  128.7 1.3 %copy-start = (bf16[8,256,512]{2,1,0:T(8,128)(2,1)}, bf16[8,256,512]{2,1,0:T(8,128)(2,1)S(1)}, u32[]{:S(2)}) copy-start(bf16[8,256,512]{2,1,0:T(8,128)(2,1)S(1)} %constant_dynamic-update-slice_fusion.1) | copy-start | bytes 6291460
